TPU v7x, 256 devices: a whole 4x4x8 slice. The times are simulated.
256 devices in a mesh: gx: 16 (over z, x_lo), gy: 16 (over y, x_hi, core).
Axes of the slice: x: 4 (x_hi: 2, x_lo: 2; x = x_hi * 2 + x_lo), y: 4, z: 8, core: 2. Of those that a mesh axis runs over, the one named last changes fastest.
Arguments:
- gradient: float32 [2048, 512], P('gx', 'gy'), may hold values from -6 to 6
- stat_old: float32 [2048, 2048], P('gx', 'gy'), may hold values from -1.001 to 1.001, as said below
Outputs:
- statistic: float32 [2048, 2048], P('gx', 'gy')
- inverse_root: float32 [2048, 2048], P('gx', 'gy')
Inputs may be any that keep to these rules, and one draw needn't show every extreme that they name: stat_old is symmetric positive semidefinite with unit diagonal, the Gram matrix of 2048 unit-length rows of 512 entries.
All inputs are finite; a program needn't handle non-finite values.
Results may differ from a plain program's by a relative error of at most 0.0003.
Values sent between devices are 32-bit elements.
A program may use at most 64 MiB of HBM per device.

v0:
```python
import jax
import jax.numpy as jnp
from jax import lax
from jax.sharding import Mesh
from jax.sharding import PartitionSpec as P

GY = ("gy_0", "gy_1", "gy_2")
GX = ("gx_0", "gx_1")
GX_GY = ("gx_0", "gx_1", "gy_0", "gy_1", "gy_2")


def gather_axes(array, axes, dim):
    filled = array
    for number in range(len(axes) - 1, -1, -1):
        filled = lax.all_gather(filled, axes[number], axis=dim, tiled=True)
    return filled


def folded(array, axes, dim, take_in, carry):
    everything = jax.tree.map(lambda part: gather_axes(part, axes, dim), array)
    return take_in(carry, everything, jnp.int32(0))


def spread(array, axes, root):
    array = jnp.where(lax.axis_index(axes) == root, array, jnp.zeros_like(array))
    for axis in axes:
        array = lax.psum(array, axis)
    return array


def over_axes(array, axes):
    for axis in axes:
        array = lax.psum(array, axis)
    return array


def matmul(leading, trailing):
    return jnp.dot(
        leading, trailing, preferred_element_type=jnp.float32, precision=lax.Precision.HIGHEST
    )


def panels(factor_one, factor_two):
    whole_row = lax.all_gather(factor_one, GY, axis=1, tiled=True)

    def accumulate(running, shard_rows, first_row):
        matching = lax.dynamic_slice_in_dim(whole_row, first_row, shard_rows.shape[0], 1)
        return running + matmul(matching, shard_rows)

    empty = jnp.zeros((factor_one.shape[0], factor_two.shape[1]), jnp.float32)
    return folded(factor_two, GX, 0, accumulate, empty)


def product(factor_one, factor_two):
    return panels(factor_one, factor_two)


def local(gradient, stat_old):
    count_rows = lax.axis_size(GX)
    count_cols = lax.axis_size(GY)
    factor = count_rows // count_cols
    piece_width = stat_old.shape[0]
    row_index = lax.axis_index(GX)
    col_index = lax.axis_index(GY)
    panel_rows = lax.all_gather(gradient, GY, axis=1, tiled=True)
    outer_parts = []
    for member in range(factor):
        column_rows = spread(panel_rows, GX, col_index * factor + member)
        outer_parts.append(matmul(panel_rows, column_rows.T))
    outer = jnp.concatenate(outer_parts, axis=1) / panel_rows.shape[1]
    statistic = 0.9 * stat_old + outer
    squares = over_axes(jnp.sum(statistic * statistic), GX_GY)
    divisor = 2.0 * jnp.sqrt(squares / (piece_width * count_rows))
    global_rows = row_index * piece_width + lax.broadcasted_iota(jnp.int32, stat_old.shape, 0)
    global_cols = col_index * (factor * piece_width) + lax.broadcasted_iota(
        jnp.int32, stat_old.shape, 1
    )
    identity = (global_rows == global_cols).astype(jnp.float32)
    normed = statistic / divisor
    first_step = 1.5 * identity - 0.5 * normed
    root_half = product(normed, first_step)
    product_mid = product(first_step, root_half)
    second_step = 1.5 * identity - 0.5 * product_mid
    inverse_root = product(second_step, first_step)
    return (statistic, inverse_root)


def solution(mesh):
    torus = Mesh(mesh.devices.reshape(8, 2, 4, 2, 2), ("gx_0", "gx_1", "gy_0", "gy_1", "gy_2"))
    placed = (P(GX, GY), P(GX, GY))
    return jax.shard_map(
        local, mesh=torus, in_specs=placed, out_specs=(P(GX, GY), P(GX, GY)), check_vma=False
    )
```

profile of v0, /device:TPU:1, one launch (start us, length us, event | category | flops | bytes accessed | tf_op | source)
XLA Modules:
  0.0 436.5 jit_solution(8363940582427046131)
XLA Ops:
  7.2 0.0 all-reduce.3.cloned.1.call-start
  7.2 0.7 copy-done.3
  7.9 26.8 %all_gather.26 = f32[128,512]{0,1:T(8,128)S(1)} all-gather(f32[128,32]{0,1:T(8,128)S(1)} %copy-done.3), channel_id=1, replica_groups=mesh['gx_0'=8,'gx_1'=2,'gy_0'=4,'gy_1'=2,'gy_2'=2] {'gy_0','gy_1','gy_2'}, dimensions={1}, use_global_device_ids=true | all-gather | bytes 278528 | tf_op jit(solution)/shard_map/all_gather | solution.py:65
  34.7 0.7 broadcast_select_fusion
  35.4 0.0 all-reduce.5.cloned.1.call-start
  35.4 65.4 %all-reduce.3.cloned.1.call-done = f32[128,512]{0,1:T(8,128)} async-done(((f32[128,512]{0,1:T(8,128)}), f32[128,512]{0,1:T(8,128)}) %all-reduce.3.cloned.1.call-update) | async-done | bytes 262160 | tf_op jit(solution)/shard_map/psum | solution.py:27
  100.9 0.0 all-gather.10.cloned.1.call-start
  100.9 0.8 copy-done.2
  101.7 0.1 copy.4
  101.8 39.7 %all-reduce.5.cloned.1.call-done = f32[128,512]{0,1:T(8,128)} async-done(((f32[128,512]{0,1:T(8,128)}), f32[128,512]{0,1:T(8,128)}) %all-reduce.5.cloned.1.call-update) | async-done | bytes 262160 | tf_op jit(solution)/shard_map/psum | solution.py:27
  141.4 2.1 multiply_reduce_fusion
  143.6 14.5 %psum.51 = f32[]{:T(128)} all-reduce(f32[]{:T(128)} %get-tuple-element.6), channel_id=1, replica_groups=mesh['gx_0'=8,'gx_1'=2,'gy_0'=4,'gy_1'=2,'gy_2'=2] {'gx_0'}, use_global_device_ids=true, to_apply=%region_3.4 | all-reduce | flops 1 | bytes 8 | tf_op jit(solution)/shard_map/psum | solution.py:33
  158.0 4.4 %psum.52 = f32[]{:T(128)} all-reduce(f32[]{:T(128)} %psum.51), channel_id=1, replica_groups=mesh['gx_0'=8,'gx_1'=2,'gy_0'=4,'gy_1'=2,'gy_2'=2] {'gx_1'}, use_global_device_ids=true, to_apply=%region_4.5 | all-reduce | flops 1 | bytes 8 | tf_op jit(solution)/shard_map/psum | solution.py:33
  162.4 9.1 %psum.53 = f32[]{:T(128)} all-reduce(f32[]{:T(128)} %psum.52), channel_id=1, replica_groups=mesh['gx_0'=8,'gx_1'=2,'gy_0'=4,'gy_1'=2,'gy_2'=2] {'gy_0'}, use_global_device_ids=true, to_apply=%region_5.6 | all-reduce | flops 1 | bytes 8 | tf_op jit(solution)/shard_map/psum | solution.py:33
  171.5 5.9 %psum.54 = f32[]{:T(128)} all-reduce(f32[]{:T(128)} %psum.53), channel_id=1, replica_groups=mesh['gx_0'=8,'gx_1'=2,'gy_0'=4,'gy_1'=2,'gy_2'=2] {'gy_1'}, use_global_device_ids=true, to_apply=%region_6.7 | all-reduce | flops 1 | bytes 8 | tf_op jit(solution)/shard_map/psum | solution.py:33
  177.4 11.8 %psum.55 = f32[]{:T(128)} all-reduce(f32[]{:T(128)} %psum.54), channel_id=1, replica_groups=mesh['gx_0'=8,'gx_1'=2,'gy_0'=4,'gy_1'=2,'gy_2'=2] {'gy_2'}, use_global_device_ids=true, to_apply=%region_7.8 | all-reduce | flops 1 | bytes 8 | tf_op jit(solution)/shard_map/psum | solution.py:33
  189.9 0.6 select_subtract_fusion
  190.5 3.9 all_gather.29
  194.4 0.0 all-gather.8.cloned.1.call-start
  194.5 0.5 all-gather.8.cloned.1.call-update
  195.0 0.5 all-gather.6.cloned.1.call-update
  195.6 29.4 %all-gather.10.cloned.1.call-done = f32[2048,128]{0,1:T(8,128)} async-done(((f32[256,128]{0,1:T(8,128)}), f32[2048,128]{0,1:T(8,128)}) %all-gather.10.cloned.1.call-update) | async-done | bytes 1048592 | tf_op jit(solution)/shard_map/all_gather | solution.py:15
  225.0 57.2 %all-gather.8.cloned.1.call-done = f32[128,2048]{0,1:T(8,128)} async-done(((f32[128,128]{0,1:T(8,128)}), f32[128,2048]{0,1:T(8,128)}) %all-gather.8.cloned.1.call-update) | async-done | bytes 1048592 | tf_op jit(solution)/shard_map/all_gather | solution.py:44
  282.2 3.4 fusion.3
  285.6 3.9 all_gather.31
  289.5 0.0 all-gather.14.cloned.1.call-start
  289.6 44.7 %all-gather.6.cloned.1.call-done = f32[128,2048]{0,1:T(8,128)} async-done(((f32[128,128]{0,1:T(8,128)}), f32[128,2048]{0,1:T(8,128)}) %all-gather.6.cloned.1.call-update) | async-done | bytes 1048592 | tf_op jit(solution)/shard_map/all_gather | solution.py:44
  334.2 33.6 %all-gather.12.cloned.1.call-done = f32[2048,128]{1,0:T(8,128)} async-done(((f32[256,128]{1,0:T(8,128)}), f32[2048,128]{1,0:T(8,128)}) %all-gather.12.cloned.1.call-update) | async-done | bytes 1048592 | tf_op jit(solution)/shard_map/all_gather | solution.py:15
  367.8 4.0 fusion
  371.8 0.7 copy.5
  372.5 53.4 %all-gather.14.cloned.1.call-done = f32[128,2048]{0,1:T(8,128)} async-done(((f32[128,128]{0,1:T(8,128)}), f32[128,2048]{0,1:T(8,128)}) %all-gather.14.cloned.1.call-update) | async-done | bytes 1048592 | tf_op jit(solution)/shard_map/all_gather | solution.py:44
  426.0 3.7 fusion.4
  (14 shorter events, 0.2 us)
Async XLA Ops:
  7.2 0.7 copy-start.3
  7.2 93.7 %all-reduce.3.cloned.1.call-start = ((), (), s32[]{:S(2)}) async-start(), calls=%async_computation | async-start | bytes 524288 | tf_op jit(solution)/shard_map/psum | solution.py:27
  35.4 106.0 %all-reduce.5.cloned.1.call-start = ((), (), s32[]{:S(2)}) async-start(), calls=%async_computation.1 | async-start | bytes 524288 | tf_op jit(solution)/shard_map/psum | solution.py:27
  100.8 0.8 copy-start.2
  100.9 124.2 %all-gather.10.cloned.1.call-start = ((), (), s32[]{:S(2)}) async-start(), calls=%async_computation.4 | async-start | bytes 1179648 | tf_op jit(solution)/shard_map/all_gather | solution.py:15
  190.5 3.9 copy-start.1
  194.4 87.8 %all-gather.8.cloned.1.call-start = ((), (), s32[]{:S(2)}) async-start(), calls=%async_computation.3 | async-start | bytes 1114112 | tf_op jit(solution)/shard_map/all_gather | solution.py:44
  195.0 139.2 %all-gather.6.cloned.1.call-start = ((), (), s32[]{:S(2)}) async-start(), calls=%async_computation.2 | async-start | bytes 1114112 | tf_op jit(solution)/shard_map/all_gather | solution.py:44
  195.6 172.2 %all-gather.12.cloned.1.call-start = ((), (), s32[]{:S(2)}) async-start(), calls=%async_computation.5 | async-start | bytes 1179648 | tf_op jit(solution)/shard_map/all_gather | solution.py:15
  289.5 136.5 %copy-start = (f32[2048,128]{0,1:T(8,128)S(1)}, f32[2048,128]{0,1:T(8,128)}, u32[]{:S(2)}) copy-start(f32[2048,128]{0,1:T(8,128)} %all-gather.10.cloned.1.call-done) | copy-start | bytes 3145732
  289.5 136.5 %all-gather.14.cloned.1.call-start = ((), (), s32[]{:S(2)}) async-start(), calls=%async_computation.6 | async-start | bytes 1114112 | tf_op jit(solution)/shard_map/all_gather | solution.py:44
Sparse Core Ops, SparseCore 0:
  35.5 65.2 all-reduce.2
  103.4 37.9 all-reduce.4
  194.5 30.4 all-gather.9
  228.2 53.9 all-gather.7
  285.4 48.7 all-gather.5
  335.9 31.8 all-gather.11
  371.9 53.9 all-gather.13
where the time goes:
time: 437 us; the launch traced here: 436 us
  waiting for transfers between devices  324 us (74%)
  blocking collectives  80.1 us (18%)
  between operations  14.9 us (3%)
  matrix products  13.2 us (3%)
    all_gather x3, waiting for transfers between devices, panels(): whole_row = lax.all_gather(factor_one, GY, axis=1, tiled=True)  155 us
    psum x2, waiting for transfers between devices, spread(): array = lax.psum(array, axis)  105 us
    all_gather x2, waiting for transfers between devices, gather_axes(): filled = lax.all_gather(filled, axes[number], axis=dim, tiled=True)  63 us
    psum x5, blocking collectives, over_axes(): array = lax.psum(array, axis)  45.6 us
    all_gather x1, blocking collectives, local(): panel_rows = lax.all_gather(gradient, GY, axis=1, tiled=True)  26.8 us
    dot_general x4, matrix products, matmul(): jnp.dot(leading, trailing, preferred_element_type=jnp.float32, precision=...  13.2 us
  transfers between devices with their start and end apart: 7, of which 7 were waited for; matrix products, arithmetic and copies ran while one was open for 1% of the time, Pallas kernels for 0%

commit v1 on v0

v1 whole, which is shorter than its diff:
```python
import functools

import jax
import jax.numpy as jnp
from jax import lax
from jax.experimental import pallas as pl
from jax.experimental.pallas import tpu as pltpu
from jax.sharding import Mesh
from jax.sharding import PartitionSpec as P

MESH = pl.DeviceIdType.MESH
GX = ("z", "a")
GY = ("y", "b", "c")
B = 128
HALF = 64
PAD = 8
KP = 32
N = 16

A0, A1, A2, A3, A4 = 2.25, -2.4375, 1.6875, -0.5625, 0.0625


def split(x):
    hi = x.astype(jnp.bfloat16)
    lo = (x - hi.astype(jnp.float32)).astype(jnp.bfloat16)
    return hi, lo


def fold4(full):
    return (full[:B, :B] + full[B:, :B]) + (full[:B, B:] + full[B:, B:])


def kernel(
    g_hbm, a_hbm, s_out, r_out,
    a_in, gt, GI, GJ, R1, C1, R2, C2,
    in_sem, gi_sem, gj_sem, gs_sem, r1_sem, c1_sem, r2_sem, c2_sem, send_sem,
):
    z, a = lax.axis_index("z"), lax.axis_index("a")
    y, b, c = lax.axis_index("y"), lax.axis_index("b"), lax.axis_index("c")
    gi = z * 2 + a
    gj = y * 4 + b * 2 + c
    a1, b1, c1 = 1 - a, 1 - b, 1 - c
    off_diag = gi != gj

    load_g = pltpu.make_async_copy(g_hbm, gt, in_sem.at[0])
    load_a = pltpu.make_async_copy(a_hbm, a_in, in_sem.at[1])
    load_g.start()
    load_a.start()

    def gx_of(s):
        i = lax.rem(gi + s, N)
        return i // 2, lax.rem(i, 2)

    def gy_of(j):
        return j // 4, lax.rem(j // 2, 2), lax.rem(j, 2)

    barrier = pltpu.get_barrier_semaphore()

    def greet(**where):
        pl.semaphore_signal(barrier, inc=1, device_id=where, device_id_type=MESH)

    zj, aj = gj // 2, lax.rem(gj, 2)

    @pl.when(off_diag)
    def _():
        for k in range(N):
            greet(z=zj, a=aj, y=k // 4, b=(k // 2) % 2, c=k % 2)

    for s in range(1, N):
        py, pb, pc = gy_of(lax.rem(gj + s, N))
        greet(y=py, b=pb, c=pc)
    up, down = lax.rem(z + 1, 8), lax.rem(z + 7, 8)
    greet(z=up)
    greet(z=down)
    greet(a=a1)

    load_g.wait()
    GI[gj] = gt[...]
    pl.semaphore_wait(barrier, 33)

    sends = []

    def send(src, dst, rsem, **where):
        copy = pltpu.make_async_remote_copy(
            src_ref=src, dst_ref=dst, send_sem=send_sem.at[len(sends)], recv_sem=rsem,
            device_id=where, device_id_type=MESH,
        )
        copy.start()
        sends.append(copy)

    def arrived(ref, rsem):
        pltpu.make_async_remote_copy(
            src_ref=ref, dst_ref=ref, send_sem=gs_sem, recv_sem=rsem,
            device_id={"a": a1}, device_id_type=MESH,
        ).wait_recv()

    iy, ib, ic = gy_of(gi)
    for s in (8, 7, 9, 6, 10, 5, 11, 4, 12, 3, 13, 2, 14, 1, 15):
        pz, pa = gx_of(s)
        send(gt, GJ.at[gj], gj_sem.at[gj], z=pz, a=pa, y=iy, b=ib, c=ic)
    for s in (8, 7, 9, 6, 10, 5, 11, 4, 12, 3, 13, 2, 14, 1, 15):
        py, pb, pc = gy_of(lax.rem(gj + s, N))
        send(gt, GI.at[gj], gi_sem.at[gj], y=py, b=pb, c=pc)

    for s in range(1, N):
        k = lax.rem(gj + s, N)
        arrived(GI.at[k], gi_sem.at[k])

    @pl.when(off_diag)
    def _():
        for k in range(N):
            arrived(GJ.at[k], gj_sem.at[k])

    @pl.when(jnp.logical_not(off_diag))
    def _():
        GJ[...] = GI[...]

    load_a.wait()
    left = jnp.transpose(GI[...].reshape(N * KP, B))
    right = GJ[...].reshape(N * KP, B)
    lh, ll = split(left)
    rh, rl = split(right)
    full = jnp.dot(
        jnp.concatenate([lh, ll], axis=0), jnp.concatenate([rh, rl], axis=1),
        preferred_element_type=jnp.float32,
    )
    stat = 0.9 * a_in[...] + fold4(full) / float(N * KP)
    s_out[...] = stat
    R1[gj] = stat
    C1[gi] = stat

    def exchange(R, C, rsem, csem, rows):
        parts = ((0, HALF), (HALF, rows - HALF))

        def row_ref(dy, bb, cc):
            k = lax.rem(y + dy, 4) * 4 + bb * 2 + cc
            return R.at[k], rsem.at[k]

        def col_ref(dz, aa, h):
            k = lax.rem(z + dz + 8, 8) * 2 + aa
            return C.at[k, pl.ds(*parts[h])], csem.at[k, h]

        def fwd(item, **where):
            ref, sem = item
            send(ref, ref, sem, **where)

        def got(item):
            arrived(*item)

        mine = row_ref(0, b, c)
        for h in (0, 1):
            fwd(col_ref(0, a, h), z=up)
            fwd(col_ref(0, a, h), z=down)
            fwd(col_ref(0, a, h), a=a1)
        fwd(mine, b=b1)
        fwd(mine, y=lax.rem(y + 1, 4))
        fwd(mine, y=lax.rem(y + 3, 4))
        fwd(mine, y=lax.rem(y + 2, 4))
        fwd(mine, c=c1)

        for h in (0, 1):
            got(col_ref(-1, a, h))
            fwd(col_ref(-1, a, h), z=up)
            got(col_ref(1, a, h))
            fwd(col_ref(1, a, h), z=down)
            got(col_ref(0, a1, h))
            fwd(col_ref(0, a1, h), z=up)
            fwd(col_ref(0, a1, h), z=down)
        for dy in (1, 3):
            got(row_ref(dy, b, c))
            fwd(row_ref(dy, b, c), c=c1)
        got(row_ref(0, b1, c))
        fwd(row_ref(0, b1, c), y=lax.rem(y + 1, 4))
        fwd(row_ref(0, b1, c), y=lax.rem(y + 3, 4))
        fwd(row_ref(0, b1, c), y=lax.rem(y + 2, 4))
        fwd(row_ref(0, b1, c), c=c1)
        for h in (0, 1):
            got(col_ref(-2, a, h))
            fwd(col_ref(-2, a, h), z=up)
            got(col_ref(2, a, h))
            fwd(col_ref(2, a, h), z=down)
            got(col_ref(-1, a1, h))
            fwd(col_ref(-1, a1, h), z=up)
            got(col_ref(1, a1, h))
            fwd(col_ref(1, a1, h), z=down)
        got(row_ref(2, b, c))
        fwd(row_ref(2, b, c), c=c1)
        for h in (0, 1):
            got(col_ref(-3, a, h))
            if h == 0:
                fwd(col_ref(-3, a, h), z=up)
            fwd(col_ref(-3, a, h), a=a1)
            got(col_ref(3, a, h))
            if h == 1:
                fwd(col_ref(3, a, h), z=down)
            fwd(col_ref(3, a, h), a=a1)
        for dy in (1, 3, 2):
            got(row_ref(dy, b1, c))
            fwd(row_ref(dy, b1, c), c=c1)
        for h in (0, 1):
            got(col_ref(4, a, h))
            fwd(col_ref(4, a, h), a=a1)
        for dy, bb in ((0, b), (1, b), (3, b), (0, b1), (2, b), (1, b1), (3, b1), (2, b1)):
            got(row_ref(dy, bb, c1))
        for dz in (-2, 2):
            for h in (0, 1):
                got(col_ref(dz, a1, h))
        for dz in (-3, 3, 4):
            for h in (0, 1):
                got(col_ref(dz, a1, h))

    exchange(R1, C1, r1_sem, c1_sem, B)

    def strips(R, k):
        rows = jnp.concatenate([R[2 * k], R[2 * k + 1]], axis=1)
        hi, lo = split(rows)
        return jnp.concatenate([hi, lo], axis=0)

    def columns(C, k):
        rows = jnp.concatenate([C[2 * k, :B], C[2 * k + 1, :B]], axis=0)
        hi, lo = split(rows)
        return jnp.concatenate([hi, lo], axis=1)

    squares = jnp.zeros((PAD, B), jnp.float32)
    total = jnp.zeros((2 * B, 2 * B), jnp.float32)
    for k in range(8):
        total = total + jnp.dot(strips(R1, k), columns(C1, k), preferred_element_type=jnp.float32)
    for k in range(N):
        block = R1[k]
        squares = squares + jnp.sum((block * block).reshape(B // PAD, PAD, B), axis=0)
    mid = fold4(total)
    R2[gj] = mid
    C2[gi, :B] = mid
    C2[gi, B:] = squares

    exchange(R2, C2, r2_sem, c2_sem, B + PAD)

    wide = jnp.zeros((2 * B, 4 * B), jnp.float32)
    for k in range(8):
        both = jnp.concatenate([columns(C1, k), columns(C2, k)], axis=1)
        wide = wide + jnp.dot(strips(R2, k), both, preferred_element_type=jnp.float32)
    cube = fold4(wide[:, : 2 * B])
    quad = fold4(wide[:, 2 * B:])
    squares = jnp.zeros((PAD, B), jnp.float32)
    for k in range(N):
        squares = squares + C2[k, B:]
    whole = jnp.sum(squares, keepdims=True)
    inv = 1.0 / (2.0 * jnp.sqrt(whole / float(N * B)))
    rows = lax.broadcasted_iota(jnp.int32, (B, B), 0) + gi * B
    cols = lax.broadcasted_iota(jnp.int32, (B, B), 1) + gj * B
    eye = jnp.where(rows == cols, A0, 0.0)
    tail = A2 * R2[gj] + inv * (A3 * cube + inv * (A4 * quad))
    r_out[...] = eye + inv * (A1 * R1[gj] + inv * tail)

    for copy in sends:
        copy.wait_send()


def local(gradient, stat_old):
    f32 = jnp.float32
    dma = pltpu.SemaphoreType.DMA
    return pl.pallas_call(
        kernel,
        out_shape=(jax.ShapeDtypeStruct((B, B), f32), jax.ShapeDtypeStruct((B, B), f32)),
        in_specs=[pl.BlockSpec(memory_space=pl.ANY)] * 2,
        out_specs=[pl.BlockSpec(memory_space=pltpu.VMEM)] * 2,
        scratch_shapes=[
            pltpu.VMEM((B, B), f32),
            pltpu.VMEM((KP, B), f32),
            pltpu.VMEM((N, KP, B), f32),
            pltpu.VMEM((N, KP, B), f32),
            pltpu.VMEM((N, B, B), f32),
            pltpu.VMEM((N, B, B), f32),
            pltpu.VMEM((N, B, B), f32),
            pltpu.VMEM((N, B + PAD, B), f32),
            dma((2,)),
            dma((N,)),
            dma((N,)),
            dma,
            dma((N,)),
            dma((N, 2)),
            dma((N,)),
            dma((N, 2)),
            dma((128,)),
        ],
        compiler_params=pltpu.CompilerParams(collective_id=0, has_side_effects=True),
    )(gradient.T, stat_old)


def solution(mesh):
    torus = Mesh(mesh.devices.reshape(8, 2, 4, 2, 2), ("z", "a", "y", "b", "c"))
    return jax.shard_map(
        local, mesh=torus, in_specs=(P(GX, GY), P(GX, GY)),
        out_specs=(P(GX, GY), P(GX, GY)), check_vma=False,
    )
```

time: 437 us -> 63.3 us (0.14)
  the two profiles are of different devices: /device:TPU:1 before, /device:TPU:32 now
where the time goes in v1:
time: 63.3 us; the launch traced here: 63.1 us
  Pallas kernels  60.4 us (95%)
  local copies, waits for them, and re-layouts  2.14 us (3%)
  between operations  0.65 us (1%)
    pallas_call x1, Pallas kernels, local(): pl.pallas_call(kernel, out_shape=(jax.ShapeDtypeStruct((B, B), f32), jax....  60.4 us
    unnamed x4, local copies, waits for them, and re-layouts  2.14 us

profile of v1, /device:TPU:32, one launch (start us, length us, event | category | flops | bytes accessed | tf_op | source)
XLA Modules:
  0.0 63.1 jit_solution(10114512285971688091)
XLA Ops:
  0.6 60.4 %shard_map.41 = (f32[128,128]{1,0:T(8,128)}, f32[128,128]{1,0:T(8,128)}) custom-call(f32[32,128]{1,0:T(8,128)} %bitcast.1, f32[128,128]{1,0:T(8,128)} %a_hbm.1), custom_call_target="tpu_custom_call" | custom-call | tf_op jit(solution)/shard_map/pallas_call | solution.py:262
  61.0 0.0 copy-start
  61.0 1.5 %copy.6 = f32[128,128]{1,0:T(8,128)} copy(f32[128,128]{1,0:T(8,128)} %get-tuple-element.4) | data formatting | bytes 131072
  62.5 0.0 copy-done
  62.5 0.6 copy.7
Async XLA Ops:
  61.0 1.5 %copy-start = (f32[128,128]{1,0:T(8,128)S(1)}, f32[128,128]{1,0:T(8,128)}, u32[]{:S(2)}) copy-start(f32[128,128]{1,0:T(8,128)} %get-tuple-element.5) | copy-start | bytes 196612

commit v2 on v1

--- a/solution.py
+++ b/solution.py
@@ -12,7 +12,7 @@
 GX = ("z", "a")
 GY = ("y", "b", "c")
 B = 128
-HALF = 64
+CH = 4
 PAD = 8
 KP = 32
 N = 16
@@ -69,14 +69,13 @@
     for s in range(1, N):
         py, pb, pc = gy_of(lax.rem(gj + s, N))
         greet(y=py, b=pb, c=pc)
-    up, down = lax.rem(z + 1, 8), lax.rem(z + 7, 8)
-    greet(z=up)
-    greet(z=down)
+    for dz in (1, 2, 6, 7):
+        greet(z=lax.rem(z + dz, 8))
     greet(a=a1)
 
     load_g.wait()
     GI[gj] = gt[...]
-    pl.semaphore_wait(barrier, 33)
+    pl.semaphore_wait(barrier, 35)
 
     sends = []
 
@@ -130,7 +129,10 @@
     C1[gi] = stat
 
     def exchange(R, C, rsem, csem, rows):
-        parts = ((0, HALF), (HALF, rows - HALF))
+        width = B // CH
+        parts = [(h * width, width) for h in range(CH)]
+        parts[-1] = (B - width, width + rows - B)
+        chunks = range(CH)
 
         def row_ref(dy, bb, cc):
             k = lax.rem(y + dy, 4) * 4 + bb * 2 + cc
@@ -147,66 +149,77 @@
         def got(item):
             arrived(*item)
 
+        def zs(dz):
+            return lax.rem(z + dz + 8, 8)
+
+        def ys(dy):
+            return lax.rem(y + dy, 4)
+
+        def far(item, h, sign):
+            fwd(item, z=zs(sign))
+            if (h % 2 == 0) == (sign > 0):
+                fwd(item, z=zs(2 * sign))
+
+        late = [h for h in chunks if h < CH // 2]
+        early = [h for h in chunks if h >= CH // 2]
+
+        for h in chunks:
+            fwd(col_ref(0, a, h), z=zs(2))
+            fwd(col_ref(0, a, h), z=zs(-2))
+            fwd(col_ref(0, a, h), a=a1)
+        for h in chunks:
+            fwd(col_ref(0, a, h), z=zs(1))
+            fwd(col_ref(0, a, h), z=zs(-1))
         mine = row_ref(0, b, c)
-        for h in (0, 1):
-            fwd(col_ref(0, a, h), z=up)
-            fwd(col_ref(0, a, h), z=down)
-            fwd(col_ref(0, a, h), a=a1)
         fwd(mine, b=b1)
-        fwd(mine, y=lax.rem(y + 1, 4))
-        fwd(mine, y=lax.rem(y + 3, 4))
-        fwd(mine, y=lax.rem(y + 2, 4))
+        for dy in (1, 3, 2):
+            fwd(mine, y=ys(dy))
         fwd(mine, c=c1)
 
-        for h in (0, 1):
-            got(col_ref(-1, a, h))
-            fwd(col_ref(-1, a, h), z=up)
-            got(col_ref(1, a, h))
-            fwd(col_ref(1, a, h), z=down)
+        for h in chunks:
             got(col_ref(0, a1, h))
-            fwd(col_ref(0, a1, h), z=up)
-            fwd(col_ref(0, a1, h), z=down)
+            if h in late:
+                fwd(col_ref(0, a1, h), z=zs(1))
+                fwd(col_ref(0, a1, h), z=zs(-1))
+        for h in chunks:
+            for sign in (1, -1):
+                item = col_ref(-2 * sign, a, h)
+                got(item)
+                fwd(item, a=a1)
+                far(item, h, sign)
         for dy in (1, 3):
             got(row_ref(dy, b, c))
             fwd(row_ref(dy, b, c), c=c1)
-        got(row_ref(0, b1, c))
-        fwd(row_ref(0, b1, c), y=lax.rem(y + 1, 4))
-        fwd(row_ref(0, b1, c), y=lax.rem(y + 3, 4))
-        fwd(row_ref(0, b1, c), y=lax.rem(y + 2, 4))
-        fwd(row_ref(0, b1, c), c=c1)
-        for h in (0, 1):
-            got(col_ref(-2, a, h))
-            fwd(col_ref(-2, a, h), z=up)
-            got(col_ref(2, a, h))
-            fwd(col_ref(2, a, h), z=down)
-            got(col_ref(-1, a1, h))
-            fwd(col_ref(-1, a1, h), z=up)
-            got(col_ref(1, a1, h))
-            fwd(col_ref(1, a1, h), z=down)
+        other = row_ref(0, b1, c)
+        got(other)
+        for dy in (1, 3, 2):
+            fwd(other, y=ys(dy))
+        fwd(other, c=c1)
+        for h in chunks:
+            for dz in (-1, 1):
+                got(col_ref(dz, a, h))
+                if h in early:
+                    fwd(col_ref(dz, a, h), a=a1)
         got(row_ref(2, b, c))
         fwd(row_ref(2, b, c), c=c1)
-        for h in (0, 1):
-            got(col_ref(-3, a, h))
-            if h == 0:
-                fwd(col_ref(-3, a, h), z=up)
-            fwd(col_ref(-3, a, h), a=a1)
-            got(col_ref(3, a, h))
-            if h == 1:
-                fwd(col_ref(3, a, h), z=down)
-            fwd(col_ref(3, a, h), a=a1)
+        for h in chunks:
+            for sign in (1, -1):
+                item = col_ref(-2 * sign, a1, h)
+                got(item)
+                if h in early:
+                    far(item, h, sign)
+        for h in chunks:
+            for dz in (-3, 3, 4):
+                got(col_ref(dz, a, h))
+                if h in late:
+                    fwd(col_ref(dz, a, h), a=a1)
         for dy in (1, 3, 2):
             got(row_ref(dy, b1, c))
             fwd(row_ref(dy, b1, c), c=c1)
-        for h in (0, 1):
-            got(col_ref(4, a, h))
-            fwd(col_ref(4, a, h), a=a1)
         for dy, bb in ((0, b), (1, b), (3, b), (0, b1), (2, b), (1, b1), (3, b1), (2, b1)):
             got(row_ref(dy, bb, c1))
-        for dz in (-2, 2):
-            for h in (0, 1):
-                got(col_ref(dz, a1, h))
-        for dz in (-3, 3, 4):
-            for h in (0, 1):
+        for dz in (-1, 1, -3, 3, 4):
+            for h in chunks:
                 got(col_ref(dz, a1, h))
 
     exchange(R1, C1, r1_sem, c1_sem, B)
@@ -278,10 +291,10 @@
             dma((N,)),
             dma,
             dma((N,)),
-            dma((N, 2)),
+            dma((N, CH)),
             dma((N,)),
-            dma((N, 2)),
-            dma((128,)),
+            dma((N, CH)),
+            dma((256,)),
         ],
         compiler_params=pltpu.CompilerParams(collective_id=0, has_side_effects=True),
     )(gradient.T, stat_old)

time: 63.3 us -> 56.4 us (0.89)
  the two profiles are of different devices: /device:TPU:32 before, /device:TPU:1 now
where the time goes in v2:
time: 56.4 us; the launch traced here: 56.2 us
  Pallas kernels  53.4 us (95%)
  local copies, waits for them, and re-layouts  2.14 us (4%)
  between operations  0.65 us (1%)
    pallas_call x1, Pallas kernels, local(): pl.pallas_call(kernel, out_shape=(jax.ShapeDtypeStruct((B, B), f32), jax....  53.4 us
    unnamed x4, local copies, waits for them, and re-layouts  2.14 us

profile of v2, /device:TPU:1, one launch (start us, length us, event | category | flops | bytes accessed | tf_op | source)
XLA Modules:
  0.0 56.2 jit_solution(17407616857093744870)
XLA Ops:
  0.6 53.4 %shard_map.41 = (f32[128,128]{1,0:T(8,128)}, f32[128,128]{1,0:T(8,128)}) custom-call(f32[32,128]{1,0:T(8,128)} %bitcast.1, f32[128,128]{1,0:T(8,128)} %a_hbm.1), custom_call_target="tpu_custom_call" | custom-call | tf_op jit(solution)/shard_map/pallas_call | solution.py:275
  54.0 0.0 copy-start
  54.1 1.5 %copy.6 = f32[128,128]{1,0:T(8,128)} copy(f32[128,128]{1,0:T(8,128)} %get-tuple-element.4) | data formatting | bytes 131072
  55.6 0.0 copy-done
  55.6 0.6 %copy.7 = f32[128,128]{1,0:T(8,128)} copy(f32[128,128]{1,0:T(8,128)S(1)} %copy-done) | data formatting | bytes 131072
Async XLA Ops:
  54.0 1.5 %copy-start = (f32[128,128]{1,0:T(8,128)S(1)}, f32[128,128]{1,0:T(8,128)}, u32[]{:S(2)}) copy-start(f32[128,128]{1,0:T(8,128)} %get-tuple-element.5) | copy-start | bytes 196612

commit v3 on v2

--- a/solution.py
+++ b/solution.py
@@ -274,7 +274,7 @@
     dma = pltpu.SemaphoreType.DMA
     return pl.pallas_call(
         kernel,
-        out_shape=(jax.ShapeDtypeStruct((B, B), f32), jax.ShapeDtypeStruct((B, B), f32)),
+        out_shape=(pltpu.VMEM((B, B), f32), pltpu.VMEM((B, B), f32)),
         in_specs=[pl.BlockSpec(memory_space=pl.ANY)] * 2,
         out_specs=[pl.BlockSpec(memory_space=pltpu.VMEM)] * 2,
         scratch_shapes=[

time: 56.4 us -> 54.8 us (0.972)
  local copies, waits for them, and re-layouts: 2.14 us -> 1.26 us
  Pallas kernels: 53.4 us -> 52.8 us
    unnamed x4 -> x2, local copies, waits for them, and re-layouts: 2.14 us -> 1.26 us
    pallas_call x1, Pallas kernels: 53.4 us -> 52.8 us  [local(): pl.pallas_call(kernel, out_shape=(pltpu.VMEM((B, B), f32), pltpu.VMEM((B,...]
where the time goes in v3:
time: 54.8 us; the launch traced here: 54.7 us
  Pallas kernels  52.8 us (96%)
  local copies, waits for them, and re-layouts  1.26 us (2%)
  between operations  0.64 us (1%)
    pallas_call x1, Pallas kernels, local(): pl.pallas_call(kernel, out_shape=(pltpu.VMEM((B, B), f32), pltpu.VMEM((B,...  52.8 us
    unnamed x2, local copies, waits for them, and re-layouts  1.26 us

profile of v3, /device:TPU:1, one launch (start us, length us, event | category | flops | bytes accessed | tf_op | source)
XLA Modules:
  0.0 54.7 jit_solution(8392163298479394233)
XLA Ops:
  0.6 52.8 %shard_map.41 = (f32[128,128]{1,0:T(8,128)S(1)}, f32[128,128]{1,0:T(8,128)S(1)}) custom-call(f32[32,128]{1,0:T(8,128)} %bitcast.1, f32[128,128]{1,0:T(8,128)} %a_hbm.1), custom_call_target="tpu_custom_call" | custom-call | tf_op jit(solution)/shard_map/pallas_call | solution.py:275
  53.4 0.6 %copy.6 = f32[128,128]{1,0:T(8,128)} copy(f32[128,128]{1,0:T(8,128)S(1)} %get-tuple-element.2) | data formatting | bytes 131072
  54.0 0.6 %copy.7 = f32[128,128]{1,0:T(8,128)} copy(f32[128,128]{1,0:T(8,128)S(1)} %get-tuple-element.3) | data formatting | bytes 131072

commit v4 on v3

v4 whole, which is shorter than its diff:
```python
import jax
import jax.numpy as jnp
from jax import lax
from jax.experimental import pallas as pl
from jax.experimental.pallas import tpu as pltpu
from jax.sharding import Mesh
from jax.sharding import PartitionSpec as P

MESH = pl.DeviceIdType.MESH
GX = ("z", "a")
GY = ("y", "b", "c")
B = 128
CH = 2
RH = 2
PAD = 8
KP = 32
N = 16

A0, A1, A2, A3, A4 = 2.25, -2.4375, 1.6875, -0.5625, 0.0625


def split(x):
    hi = x.astype(jnp.bfloat16)
    lo = (x - hi.astype(jnp.float32)).astype(jnp.bfloat16)
    return hi, lo


def fold4(full):
    return (full[:B, :B] + full[B:, :B]) + (full[:B, B:] + full[B:, B:])


def kernel(
    g_hbm, a_hbm, s_out, r_out,
    a_in, gt, GI, GJ, R1, C1, R2, C2, a_new, s_new, r_own, r_new,
    in_sem, gi_sem, gj_sem, gs_sem, down_sem, swap_sem, r1_sem, c1_sem, r2_sem, c2_sem, send_sem,
):
    z, a = lax.axis_index("z"), lax.axis_index("a")
    y, b, c = lax.axis_index("y"), lax.axis_index("b"), lax.axis_index("c")
    a1, b1, c1 = 1 - a, 1 - b, 1 - c
    x = 2 * b + a
    gi = z * 2 + c
    gj = y * 4 + x
    own = c * 8 + y * 2 + b
    home = z == 2 * y + b
    swaps = a != c

    load_g = pltpu.make_async_copy(g_hbm, gt, in_sem.at[0])
    load_a = pltpu.make_async_copy(a_hbm, a_in, in_sem.at[1])
    load_g.start()
    load_a.start()

    barrier = pltpu.get_barrier_semaphore()

    def greet(**where):
        pl.semaphore_signal(barrier, inc=1, device_id=where, device_id_type=MESH)

    def zs(dz):
        return lax.rem(z + dz + 8, 8)

    def ys(dy):
        return lax.rem(y + dy + 4, 4)

    def xs(dx):
        to = lax.rem(x + dx + 4, 4)
        return {"b": to // 2, "a": lax.rem(to, 2)}

    def place(slot):
        return {"y": (slot % 8) // 2, "b": slot % 2, "c": slot // 8}

    @pl.when(c == 0)
    def _():
        for slot in range(N):
            @pl.when(jnp.logical_not(jnp.logical_and(home, own == slot)))
            def _():
                greet(z=2 * y + b, **place(slot))

    for slot in range(N):
        @pl.when(jnp.logical_not(jnp.logical_and(a == c, own == slot)))
        def _():
            greet(a=c, **place(slot))

    @pl.when(swaps)
    def _():
        greet(a=a1, c=c1)

    @pl.when(c == 1)
    def _():
        greet(c=0)

    for dz in (2, -2, 1, -1):
        greet(z=zs(dz))
    for d in (2, 1, -1):
        greet(y=ys(d))
        greet(**xs(d))
    greet(c=c1)
    alike = jnp.where(a == c, 1, 0)
    at_home = jnp.where(home, 1, 0)
    expected = 36 - 2 * alike + (1 - c) - (1 - c) * at_home

    load_g.wait()
    pl.semaphore_wait(barrier, expected)

    sends = []

    def send(src, dst, rsem, cond=None, **where):
        copy = pltpu.make_async_remote_copy(
            src_ref=src, dst_ref=dst, send_sem=send_sem.at[len(sends)], recv_sem=rsem,
            device_id=where, device_id_type=MESH,
        )
        if cond is None:
            copy.start()
        else:
            pl.when(cond)(copy.start)
        sends.append((copy, cond))

    def arrived(ref, rsem):
        pltpu.make_async_remote_copy(
            src_ref=ref, dst_ref=ref, send_sem=gs_sem, recv_sem=rsem,
            device_id={"c": c1}, device_id_type=MESH,
        ).wait_recv()

    col_y, col_b = z // 2, lax.rem(z, 2)
    for dz in (4, 3, 5, 2, 6, 1, 7):
        send(gt, GJ.at[own], gj_sem.at[own], z=zs(dz), y=col_y, b=col_b, c=0)
    away = jnp.logical_not(jnp.logical_and(home, c == 0))
    send(gt, GJ.at[own], gj_sem.at[own], away, y=col_y, b=col_b, c=0)
    for dx in (2, 1, -1, 0):
        for dy in (2, 1, -1, 0):
            cond = swaps if dx == 0 and dy == 0 else None
            to = xs(dx)
            send(gt, GI.at[own], gi_sem.at[own], cond, y=ys(dy), b=to["b"], a=to["a"], c=a)

    load_a.wait()
    send(a_in, a_new, swap_sem.at[0], swaps, a=a1, c=c1)

    @pl.when(a == c)
    def _():
        GI[own] = gt[...]
        a_new[...] = a_in[...]

    @pl.when(jnp.logical_and(home, c == 0))
    def _():
        GJ[own] = gt[...]

    lower = GJ.at[pl.ds(0, 8)]
    upper = GJ.at[pl.ds(8, 8)]
    for group, part in enumerate((lower, upper)):
        @pl.when(c == 0)
        def _():
            for slot in range(8 * group, 8 * group + 8):
                @pl.when(jnp.logical_not(jnp.logical_and(home, own == slot)))
                def _():
                    arrived(GJ.at[slot], gj_sem.at[slot])

        send(part, part, down_sem.at[group], c == 0, c=c1)

    for t in range(1, N):
        slot = lax.rem(own + t, N)
        arrived(GI.at[slot], gi_sem.at[slot])

    @pl.when(swaps)
    def _():
        arrived(GI.at[own], gi_sem.at[own])
        arrived(a_new, swap_sem.at[0])

    @pl.when(c == 1)
    def _():
        arrived(lower, down_sem.at[0])
        arrived(upper, down_sem.at[1])

    left = jnp.transpose(GI[...].reshape(N * KP, B))
    right = GJ[...].reshape(N * KP, B)
    lh, ll = split(left)
    rh, rl = split(right)
    full = jnp.dot(
        jnp.concatenate([lh, ll], axis=0), jnp.concatenate([rh, rl], axis=1),
        preferred_element_type=jnp.float32,
    )
    stat = 0.9 * a_new[...] + fold4(full) / float(N * KP)
    R1[gj] = stat
    C1[gi] = stat

    def exchange(R, C, rsem, csem, rows, extra):
        width = B // CH
        parts = [(h * width, width) for h in range(CH)]
        parts[-1] = (B - width, width + rows - B)
        chunks = range(CH)
        tall = B // RH
        pairs = [(h, h + RH // 2) for h in range(RH // 2)]

        def row_ref(dy, dx, h):
            k = ys(dy) * 4 + lax.rem(x + dx + 4, 4)
            return R.at[k, pl.ds(h * tall, tall)], rsem.at[k, h]

        def col_ref(dz, core, h):
            k = zs(dz) * 2 + core
            return C.at[k, pl.ds(*parts[h])], csem.at[k, h]

        def fwd(item, **where):
            ref, sem = item
            send(ref, ref, sem, **where)

        def got(item):
            arrived(*item)

        for dz in (2, -2, 1, -1):
            for h in chunks:
                fwd(col_ref(0, c, h), z=zs(dz))
        for h, v in pairs:
            for d in (2, 1, -1):
                fwd(row_ref(0, 0, h), **xs(d))
                fwd(row_ref(0, 0, v), y=ys(d))
        for h in chunks:
            fwd(col_ref(0, c, h), c=c1)
        for h, v in pairs:
            for d in (2, 1, -1):
                fwd(row_ref(0, 0, v), **xs(d))
                fwd(row_ref(0, 0, h), y=ys(d))
        extra()

        for h, v in pairs:
            for d in (1, -1, 2):
                got(row_ref(0, d, h))
                for e in (2, 1, -1):
                    fwd(row_ref(0, d, h), y=ys(e))
                got(row_ref(d, 0, v))
                for e in (2, 1, -1):
                    fwd(row_ref(d, 0, v), **xs(e))
        for h in chunks:
            for sign in (1, -1):
                item = col_ref(-2 * sign, c, h)
                got(item)
                fwd(item, z=zs(sign))
                if (h % 2 == 0) == (sign > 0):
                    fwd(item, z=zs(2 * sign))
                fwd(item, c=c1)
        for h in chunks:
            for dz in (-1, 1):
                got(col_ref(dz, c, h))
                fwd(col_ref(dz, c, h), c=c1)
        for h in chunks:
            for dz in (-3, 3, 4):
                got(col_ref(dz, c, h))
                fwd(col_ref(dz, c, h), c=c1)
        for h, v in pairs:
            for d in (1, -1, 2):
                got(row_ref(0, d, v))
                got(row_ref(d, 0, h))
                for e in (1, -1, 2):
                    got(row_ref(e, d, h))
                    got(row_ref(d, e, v))
        for h in chunks:
            for dz in (0, -1, 1, -2, 2, -3, 3, 4):
                got(col_ref(dz, c1, h))

    def give_stat():
        send(R1.at[gj], s_new, swap_sem.at[1], swaps, a=a1, c=c1)

    exchange(R1, C1, r1_sem, c1_sem, B, give_stat)

    def strips(R, k):
        rows = jnp.concatenate([R[2 * k], R[2 * k + 1]], axis=1)
        hi, lo = split(rows)
        return jnp.concatenate([hi, lo], axis=0)

    def columns(C, k):
        rows = jnp.concatenate([C[2 * k, :B], C[2 * k + 1, :B]], axis=0)
        hi, lo = split(rows)
        return jnp.concatenate([hi, lo], axis=1)

    squares = jnp.zeros((PAD, B), jnp.float32)
    total = jnp.zeros((2 * B, 2 * B), jnp.float32)
    for k in range(8):
        total = total + jnp.dot(strips(R1, k), columns(C1, k), preferred_element_type=jnp.float32)
    for k in range(N):
        block = R1[k]
        squares = squares + jnp.sum((block * block).reshape(B // PAD, PAD, B), axis=0)
    mid = fold4(total)
    R2[gj] = mid
    C2[gi, :B] = mid
    C2[gi, B:] = squares

    def keep_stat():
        @pl.when(swaps)
        def _():
            arrived(s_new, swap_sem.at[1])
            s_out[...] = s_new[...]

        @pl.when(a == c)
        def _():
            s_out[...] = R1[gj]

    exchange(R2, C2, r2_sem, c2_sem, B + PAD, keep_stat)

    wide = jnp.zeros((2 * B, 4 * B), jnp.float32)
    for k in range(8):
        both = jnp.concatenate([columns(C1, k), columns(C2, k)], axis=1)
        wide = wide + jnp.dot(strips(R2, k), both, preferred_element_type=jnp.float32)
    cube = fold4(wide[:, : 2 * B])
    quad = fold4(wide[:, 2 * B:])
    squares = jnp.zeros((PAD, B), jnp.float32)
    for k in range(N):
        squares = squares + C2[k, B:]
    whole = jnp.sum(squares, keepdims=True)
    inv = 1.0 / (2.0 * jnp.sqrt(whole / float(N * B)))
    rows = lax.broadcasted_iota(jnp.int32, (B, B), 0) + gi * B
    cols = lax.broadcasted_iota(jnp.int32, (B, B), 1) + gj * B
    eye = jnp.where(rows == cols, A0, 0.0)
    tail = A2 * R2[gj] + inv * (A3 * cube + inv * (A4 * quad))
    r_own[...] = eye + inv * (A1 * R1[gj] + inv * tail)
    send(r_own, r_new, swap_sem.at[2], swaps, a=a1, c=c1)

    @pl.when(swaps)
    def _():
        arrived(r_new, swap_sem.at[2])
        r_out[...] = r_new[...]

    @pl.when(a == c)
    def _():
        r_out[...] = r_own[...]

    for copy, cond in sends:
        if cond is None:
            copy.wait_send()
        else:
            pl.when(cond)(copy.wait_send)


def local(gradient, stat_old):
    f32 = jnp.float32
    dma = pltpu.SemaphoreType.DMA
    tile = pltpu.VMEM((B, B), f32)
    pieces = pltpu.VMEM((N, KP, B), f32)
    strip = pltpu.VMEM((N, B, B), f32)
    return pl.pallas_call(
        kernel,
        out_shape=(pltpu.VMEM((B, B), f32), pltpu.VMEM((B, B), f32)),
        in_specs=[pl.BlockSpec(memory_space=pl.ANY)] * 2,
        out_specs=[pl.BlockSpec(memory_space=pltpu.VMEM)] * 2,
        scratch_shapes=[
            tile, pltpu.VMEM((KP, B), f32), pieces, pieces,
            strip, strip, strip, pltpu.VMEM((N, B + PAD, B), f32),
            tile, tile, tile, tile,
            dma((2,)), dma((N,)), dma((N,)), dma, dma((2,)), dma((3,)),
            dma((N, RH)), dma((N, CH)), dma((N, RH)), dma((N, CH)), dma((256,)),
        ],
        compiler_params=pltpu.CompilerParams(collective_id=0, has_side_effects=True),
    )(gradient.T, stat_old)


def solution(mesh):
    torus = Mesh(mesh.devices.reshape(8, 2, 4, 2, 2), ("z", "a", "y", "b", "c"))
    return jax.shard_map(
        local, mesh=torus, in_specs=(P(GX, GY), P(GX, GY)),
        out_specs=(P(GX, GY), P(GX, GY)), check_vma=False,
    )
```

time: 54.8 us -> 52.9 us (0.965)
  Pallas kernels: 52.8 us -> 50.8 us
    pallas_call x1, Pallas kernels: 52.8 us -> 50.8 us  [local(): pl.pallas_call(kernel, out_shape=(pltpu.VMEM((B, B), f32), pltpu.VMEM((B,...]
where the time goes in v4:
time: 52.9 us; the launch traced here: 52.7 us
  Pallas kernels  50.8 us (96%)
  local copies, waits for them, and re-layouts  1.26 us (2%)
  between operations  0.64 us (1%)
    pallas_call x1, Pallas kernels, local(): pl.pallas_call(kernel, out_shape=(pltpu.VMEM((B, B), f32), pltpu.VMEM((B,...  50.8 us
    unnamed x2, local copies, waits for them, and re-layouts  1.26 us

profile of v4, /device:TPU:1, one launch (start us, length us, event | category | flops | bytes accessed | tf_op | source)
XLA Modules:
  0.0 52.7 jit_solution(17187164950802303286)
XLA Ops:
  0.6 50.8 %shard_map.41 = (f32[128,128]{1,0:T(8,128)S(1)}, f32[128,128]{1,0:T(8,128)S(1)}) custom-call(f32[32,128]{1,0:T(8,128)} %bitcast.1, f32[128,128]{1,0:T(8,128)} %a_hbm.1), custom_call_target="tpu_custom_call" | custom-call | tf_op jit(solution)/shard_map/pallas_call | solution.py:335
  51.5 0.6 %copy.6 = f32[128,128]{1,0:T(8,128)} copy(f32[128,128]{1,0:T(8,128)S(1)} %get-tuple-element.2) | data formatting | bytes 131072
  52.1 0.6 %copy.7 = f32[128,128]{1,0:T(8,128)} copy(f32[128,128]{1,0:T(8,128)S(1)} %get-tuple-element.3) | data formatting | bytes 131072

commit v5 on v4

v5 whole, which is shorter than its diff:
```python
import jax
import jax.numpy as jnp
from jax import lax
from jax.experimental import pallas as pl
from jax.experimental.pallas import tpu as pltpu
from jax.sharding import Mesh
from jax.sharding import PartitionSpec as P

MESH = pl.DeviceIdType.MESH
GX = ("z", "a")
GY = ("y", "b", "c")
B = 128
CH = 2
RH = 4
EARLY = (0, -1, 1, -2, 2)
LATE = (-3, 3, 4)
PAD = 8
KP = 32
N = 16

A0, A1, A2, A3, A4 = 2.25, -2.4375, 1.6875, -0.5625, 0.0625


def split(x):
    hi = x.astype(jnp.bfloat16)
    lo = (x - hi.astype(jnp.float32)).astype(jnp.bfloat16)
    return hi, lo


def fold4(full):
    return (full[:B, :B] + full[B:, :B]) + (full[:B, B:] + full[B:, B:])


def kernel(
    g_hbm, a_hbm, s_out, r_out,
    a_in, gt, GI, GJ, R1, C1, R2, C2, CB, a_new, s_new, r_own, r_new,
    in_sem, gi_sem, gj_sem, gs_sem, down_sem, swap_sem, piece_sem, send_sem, *gather_sems,
):
    z, a = lax.axis_index("z"), lax.axis_index("a")
    y, b, c = lax.axis_index("y"), lax.axis_index("b"), lax.axis_index("c")
    a1, b1, c1 = 1 - a, 1 - b, 1 - c
    x = 2 * b + a
    gi = z * 2 + c
    gj = y * 4 + x
    own = c * 8 + y * 2 + b
    home = z == 2 * y + b
    swaps = a != c

    sems1, sems2 = gather_sems[:7], gather_sems[7:]
    load_g = pltpu.make_async_copy(g_hbm, gt, in_sem.at[0])
    load_a = pltpu.make_async_copy(a_hbm, a_in, in_sem.at[1])
    load_g.start()
    load_a.start()

    barrier = pltpu.get_barrier_semaphore()

    def greet(**where):
        pl.semaphore_signal(barrier, inc=1, device_id=where, device_id_type=MESH)

    def zs(dz):
        return lax.rem(z + dz + 8, 8)

    def ys(dy):
        return lax.rem(y + dy + 4, 4)

    def xs(dx):
        to = lax.rem(x + dx + 4, 4)
        return {"b": to // 2, "a": lax.rem(to, 2)}

    def place(slot):
        return {"y": (slot % 8) // 2, "b": slot % 2, "c": slot // 8}

    @pl.when(c == 0)
    def _():
        for slot in range(N):
            @pl.when(jnp.logical_not(jnp.logical_and(home, own == slot)))
            def _():
                greet(z=2 * y + b, **place(slot))

    for slot in range(N):
        @pl.when(jnp.logical_not(jnp.logical_and(a == c, own == slot)))
        def _():
            greet(a=c, **place(slot))

    @pl.when(swaps)
    def _():
        greet(a=a1, c=c1)

    @pl.when(c == 1)
    def _():
        greet(c=0)

    for dz in (2, -2, 1, -1):
        greet(z=zs(dz))
    for d in (2, 1, -1):
        greet(y=ys(d))
        greet(**xs(d))
    greet(c=c1)
    alike = jnp.where(a == c, 1, 0)
    at_home = jnp.where(home, 1, 0)
    expected = 36 - 2 * alike + (1 - c) - (1 - c) * at_home

    load_g.wait()
    pl.semaphore_wait(barrier, expected)

    sends = []

    def start(src, dst, ssem, rsem, **where):
        copy = pltpu.make_async_remote_copy(
            src_ref=src, dst_ref=dst, send_sem=ssem, recv_sem=rsem,
            device_id=where, device_id_type=MESH,
        )
        copy.start()

    def send(src, dst, rsem, cond, **where):
        copy = pltpu.make_async_remote_copy(
            src_ref=src, dst_ref=dst, send_sem=send_sem.at[len(sends)], recv_sem=rsem,
            device_id=where, device_id_type=MESH,
        )
        pl.when(cond)(copy.start)
        sends.append((copy, cond))

    def left_here(ref, ssem):
        pltpu.make_async_remote_copy(
            src_ref=ref, dst_ref=ref, send_sem=ssem, recv_sem=gs_sem,
            device_id={"c": c1}, device_id_type=MESH,
        ).wait_send()

    def arrived(ref, rsem):
        pltpu.make_async_remote_copy(
            src_ref=ref, dst_ref=ref, send_sem=gs_sem, recv_sem=rsem,
            device_id={"c": c1}, device_id_type=MESH,
        ).wait_recv()

    col_y, col_b = z // 2, lax.rem(z, 2)
    for dz in (4, 3, 5, 2, 6, 1, 7):
        start(gt, GJ.at[own], piece_sem, gj_sem.at[c], z=zs(dz), y=col_y, b=col_b, c=0)
    away = jnp.logical_not(jnp.logical_and(home, c == 0))
    send(gt, GJ.at[own], gj_sem.at[c], away, y=col_y, b=col_b, c=0)
    for dx in (2, 1, -1, 0):
        for dy in (2, 1, -1, 0):
            if dx or dy:
                to = xs(dx)
                start(gt, GI.at[own], piece_sem, gi_sem, y=ys(dy), b=to["b"], a=to["a"], c=a)
    send(gt, GI.at[own], gi_sem, swaps, c=a)

    load_a.wait()
    send(a_in, a_new, swap_sem.at[0], swaps, a=a1, c=c1)

    @pl.when(a == c)
    def _():
        GI[own] = gt[...]
        a_new[...] = a_in[...]

    @pl.when(jnp.logical_and(home, c == 0))
    def _():
        GJ[own] = gt[...]

    lower = GJ.at[pl.ds(0, 8)]
    upper = GJ.at[pl.ds(8, 8)]

    @pl.when(c == 0)
    def _():
        @pl.when(home)
        def _():
            arrived(GJ.at[pl.ds(0, 7)], gj_sem.at[0])

        @pl.when(jnp.logical_not(home))
        def _():
            arrived(lower, gj_sem.at[0])

    send(lower, lower, down_sem.at[0], c == 0, c=c1)

    @pl.when(c == 0)
    def _():
        arrived(upper, gj_sem.at[1])

    send(upper, upper, down_sem.at[1], c == 0, c=c1)

    @pl.when(a == c)
    def _():
        arrived(GI.at[pl.ds(0, N - 1)], gi_sem)

    @pl.when(swaps)
    def _():
        arrived(GI, gi_sem)
        arrived(a_new, swap_sem.at[0])

    @pl.when(c == 1)
    def _():
        arrived(lower, down_sem.at[0])
        arrived(upper, down_sem.at[1])

    left = jnp.transpose(GI[...].reshape(N * KP, B))
    right = GJ[...].reshape(N * KP, B)
    lh, ll = split(left)
    rh, rl = split(right)
    full = jnp.dot(
        jnp.concatenate([lh, ll], axis=0), jnp.concatenate([rh, rl], axis=1),
        preferred_element_type=jnp.float32,
    )
    stat = 0.9 * a_new[...] + fold4(full) / float(N * KP)
    R1[gj] = stat
    C1[gi] = stat

    def exchange(R, C, sems, rows, extra, ready):
        width = B // CH
        parts = [(h * width, width) for h in range(CH)]
        parts[-1] = (B - width, width + rows - B)
        chunks = range(CH)
        tall = B // RH
        pairs = [(h, h + RH // 2) for h in range(RH // 2)]
        leg_sem, rest_sem, far_sem, block_sem, twin_sem, row_sent, col_sent = sems

        def row_ref(dy, dx, h):
            k = ys(dy) * 4 + lax.rem(x + dx + 4, 4)
            return R.at[k, pl.ds(h * tall, tall)], leg_sem.at[k, h]

        def col_ref(dz, core, h):
            k = zs(dz) * 2 + core
            return C.at[k, pl.ds(*parts[h])], far_sem.at[k, h]

        def col_block(dz):
            k = zs(dz) * 2 + c
            return C.at[k], block_sem.at[k]

        def leg(ref, sem, **where):
            start(ref, ref, row_sent, sem, **where)

        def hop(ref, sem, **where):
            start(ref, ref, col_sent, sem, **where)

        def twin(ref, dz):
            hop(ref, twin_sem.at[0 if dz in EARLY else 1], c=c1)

        for h in chunks:
            for dz in (2, -2):
                hop(*col_ref(0, c, h), z=zs(dz))
        for h in chunks:
            for dz in (1, -1):
                hop(col_ref(0, c, h)[0], col_block(0)[1], z=zs(dz))
        for h, v in pairs:
            for d in (2, 1, -1):
                leg(*row_ref(0, 0, h), **xs(d))
                leg(*row_ref(0, 0, v), y=ys(d))
        twin(col_block(0)[0], 0)
        for h, v in pairs:
            for d in (2, 1, -1):
                leg(row_ref(0, 0, v)[0], rest_sem, **xs(d))
                leg(row_ref(0, 0, h)[0], rest_sem, y=ys(d))

        for step in chunks:
            h, v = pairs[step]
            for d in (1, -1, 2):
                item = row_ref(0, d, h)
                arrived(*item)
                for e in (2, 1, -1):
                    leg(item[0], rest_sem, y=ys(e))
                item = row_ref(d, 0, v)
                arrived(*item)
                for e in (2, 1, -1):
                    leg(item[0], rest_sem, **xs(e))
            for sign in (1, -1):
                item = col_ref(-2 * sign, c, step)
                arrived(*item)
                if (step % 2 == 0) == (sign > 0):
                    hop(item[0], col_block(-2 * sign)[1], z=zs(2 * sign))
                hop(item[0], col_block(-2 * sign)[1], z=zs(sign))
                twin(item[0], -2)
        for dz in (-1, 1) + LATE:
            item = col_block(dz)
            arrived(*item)
            twin(item[0], dz)
        extra()
        arrived(R.at[pl.ds(0, 12)], rest_sem)
        arrived(C.at[pl.ds(0, len(EARLY))], twin_sem.at[0])
        ready(EARLY)
        arrived(C.at[pl.ds(0, len(LATE))], twin_sem.at[1])

    def sent(R, C, sems):
        left_here(R.at[pl.ds(0, N - 1)], sems[-2])
        left_here(C.at[pl.ds(0, N - 1)], sems[-1])

    def give_stat():
        send(R1.at[gj], s_new, swap_sem.at[1], swaps, a=a1, c=c1)

    def strips(R, k):
        return split(jnp.concatenate([R[2 * k], R[2 * k + 1]], axis=1))

    def columns(C, k):
        rows = jnp.concatenate([C[2 * k, :B], C[2 * k + 1, :B]], axis=0)
        return jnp.concatenate(split(rows), axis=1)

    total = []

    def square(steps):
        for dz in steps:
            k = zs(dz)
            CB[k] = columns(C1, k)
            total.append(jnp.dot(
                jnp.concatenate(strips(R1, k), axis=0), CB[k], preferred_element_type=jnp.float32
            ))

    exchange(R1, C1, sems1, B, give_stat, square)
    square(LATE)
    squares = jnp.zeros((PAD, B), jnp.float32)
    for k in range(N):
        block = R1[k]
        squares = squares + jnp.sum((block * block).reshape(B // PAD, PAD, B), axis=0)
    mid = fold4(sum(total[1:], total[0]))
    R2[gj] = mid
    C2[gi, :B] = mid
    C2[gi, B:] = squares

    def keep_stat():
        @pl.when(swaps)
        def _():
            arrived(s_new, swap_sem.at[1])
            s_out[...] = s_new[...]

        @pl.when(a == c)
        def _():
            s_out[...] = R1[gj]

    half = B // 2
    wide = [[], []]

    def powers(steps, halves):
        for part in halves:
            for dz in steps:
                k = zs(dz)
                both = jnp.concatenate([CB[k], columns(C2, k)], axis=1)
                hi, lo = strips(R2, k)
                cut = slice(part * half, part * half + half)
                wide[part].append(jnp.dot(
                    jnp.concatenate([hi[cut], lo[cut]], axis=0), both, preferred_element_type=jnp.float32
                ))

    exchange(R2, C2, sems2, B + PAD, keep_stat, lambda steps: powers(steps, (0, 1)))

    squares = jnp.zeros((PAD, B), jnp.float32)
    for k in range(N):
        squares = squares + C2[k, B:]
    whole = jnp.sum(squares, keepdims=True)
    inv = 1.0 / (2.0 * jnp.sqrt(whole / float(N * B)))
    rows = lax.broadcasted_iota(jnp.int32, (half, B), 0) + gi * B
    cols = lax.broadcasted_iota(jnp.int32, (half, B), 1) + gj * B

    def fold2(full):
        return (full[:half, :B] + full[half:, :B]) + (full[:half, B:] + full[half:, B:])

    for part in (0, 1):
        powers(LATE, (part,))
        full = sum(wide[part][1:], wide[part][0])
        cube = fold2(full[:, : 2 * B])
        quad = fold2(full[:, 2 * B:])
        cut = pl.ds(part * half, half)
        eye = jnp.where(rows + part * half == cols, A0, 0.0)
        tail = A2 * R2[gj, cut] + inv * (A3 * cube + inv * (A4 * quad))
        r_own[cut] = eye + inv * (A1 * R1[gj, cut] + inv * tail)
        send(r_own.at[cut], r_new.at[cut], swap_sem.at[2 + part], swaps, a=a1, c=c1)

    @pl.when(swaps)
    def _():
        for part in (0, 1):
            cut = pl.ds(part * half, half)
            arrived(r_new.at[cut], swap_sem.at[2 + part])
            r_out[cut] = r_new[cut]

    @pl.when(a == c)
    def _():
        r_out[...] = r_own[...]

    left_here(R1.at[pl.ds(0, 11), pl.ds(0, 2 * KP)], piece_sem)
    sent(R1, C1, sems1)
    sent(R2, C2, sems2)
    for copy, cond in sends:
        pl.when(cond)(copy.wait_send)


def local(gradient, stat_old):
    f32 = jnp.float32
    dma = pltpu.SemaphoreType.DMA
    tile = pltpu.VMEM((B, B), f32)
    pieces = pltpu.VMEM((N, KP, B), f32)
    strip = pltpu.VMEM((N, B, B), f32)
    gather_sems = [dma((N, RH)), dma, dma((N, CH)), dma((N,)), dma((2,)), dma, dma]
    return pl.pallas_call(
        kernel,
        out_shape=(pltpu.VMEM((B, B), f32), pltpu.VMEM((B, B), f32)),
        in_specs=[pl.BlockSpec(memory_space=pl.ANY)] * 2,
        out_specs=[pl.BlockSpec(memory_space=pltpu.VMEM)] * 2,
        scratch_shapes=[
            tile, pltpu.VMEM((KP, B), f32), pieces, pieces,
            strip, strip, strip, pltpu.VMEM((N, B + PAD, B), f32),
            pltpu.VMEM((N // 2, 2 * B, 2 * B), jnp.bfloat16),
            tile, tile, tile, tile,
            dma((2,)), dma, dma((2,)), dma, dma((2,)), dma((4,)), dma, dma((16,)),
            *gather_sems, *gather_sems,
        ],
        compiler_params=pltpu.CompilerParams(collective_id=0, has_side_effects=True),
    )(gradient.T, stat_old)


def solution(mesh):
    torus = Mesh(mesh.devices.reshape(8, 2, 4, 2, 2), ("z", "a", "y", "b", "c"))
    return jax.shard_map(
        local, mesh=torus, in_specs=(P(GX, GY), P(GX, GY)),
        out_specs=(P(GX, GY), P(GX, GY)), check_vma=False,
    )
```

time: 52.9 us -> 50.4 us (0.953)
  Pallas kernels: 50.8 us -> 48.4 us
    pallas_call x1, Pallas kernels: 50.8 us -> 48.4 us  [local(): pl.pallas_call(kernel, out_shape=(pltpu.VMEM((B, B), f32), pltpu.VMEM((B,...]
where the time goes in v5:
time: 50.4 us; the launch traced here: 50.3 us
  Pallas kernels  48.4 us (96%)
  local copies, waits for them, and re-layouts  1.26 us (2%)
  between operations  0.64 us (1%)
    pallas_call x1, Pallas kernels, local(): pl.pallas_call(kernel, out_shape=(pltpu.VMEM((B, B), f32), pltpu.VMEM((B,...  48.4 us
    unnamed x2, local copies, waits for them, and re-layouts  1.26 us

profile of v5, /device:TPU:1, one launch (start us, length us, event | category | flops | bytes accessed | tf_op | source)
XLA Modules:
  0.0 50.3 jit_solution(15914422438121968834)
XLA Ops:
  0.6 48.4 %shard_map.41 = (f32[128,128]{1,0:T(8,128)S(1)}, f32[128,128]{1,0:T(8,128)S(1)}) custom-call(f32[32,128]{1,0:T(8,128)} %bitcast.1, f32[128,128]{1,0:T(8,128)} %a_hbm.1), custom_call_target="tpu_custom_call" | custom-call | tf_op jit(solution)/shard_map/pallas_call | solution.py:388
  49.0 0.6 %copy.6 = f32[128,128]{1,0:T(8,128)} copy(f32[128,128]{1,0:T(8,128)S(1)} %get-tuple-element.2) | data formatting | bytes 131072
  49.6 0.6 %copy.7 = f32[128,128]{1,0:T(8,128)} copy(f32[128,128]{1,0:T(8,128)S(1)} %get-tuple-element.3) | data formatting | bytes 131072

commit v6 on v5

--- a/solution.py
+++ b/solution.py
@@ -68,19 +68,23 @@
         return {"b": to // 2, "a": lax.rem(to, 2)}
 
     def place(slot):
-        return {"y": (slot % 8) // 2, "b": slot % 2, "c": slot // 8}
+        return {"y": lax.rem(slot // 2, 4), "b": lax.rem(slot, 2), "c": slot // 8}
 
     @pl.when(c == 0)
     def _():
-        for slot in range(N):
-            @pl.when(jnp.logical_not(jnp.logical_and(home, own == slot)))
-            def _():
-                greet(z=2 * y + b, **place(slot))
-
-    for slot in range(N):
-        @pl.when(jnp.logical_not(jnp.logical_and(a == c, own == slot)))
+        for t in range(1, N):
+            greet(z=2 * y + b, **place(lax.rem(own + t, N)))
+
+        @pl.when(jnp.logical_not(home))
         def _():
-            greet(a=c, **place(slot))
+            greet(z=2 * y + b)
+
+    for t in range(1, N):
+        greet(a=c, **place(lax.rem(own + t, N)))
+
+    @pl.when(swaps)
+    def _():
+        greet(a=c)
 
     @pl.when(swaps)
     def _():
@@ -214,15 +218,19 @@
 
         def row_ref(dy, dx, h):
             k = ys(dy) * 4 + lax.rem(x + dx + 4, 4)
-            return R.at[k, pl.ds(h * tall, tall)], leg_sem.at[k, h]
-
-        def col_ref(dz, core, h):
-            k = zs(dz) * 2 + core
-            return C.at[k, pl.ds(*parts[h])], far_sem.at[k, h]
-
-        def col_block(dz):
-            k = zs(dz) * 2 + c
-            return C.at[k], block_sem.at[k]
+            return R.at[k, pl.ds(h * tall, tall)]
+
+        def leg_of(d, h):
+            return leg_sem.at[d % 4 - 1, h]
+
+        def col_ref(dz, h):
+            return C.at[zs(dz) * 2 + c, pl.ds(*parts[h])]
+
+        def far_of(dz, h):
+            return far_sem.at[0 if dz > 0 else 1, h]
+
+        def block_of(dz):
+            return block_sem.at[(1, -1, 3, -3, 4).index(dz)]
 
         def leg(ref, sem, **where):
             start(ref, ref, row_sent, sem, **where)
@@ -235,42 +243,42 @@
 
         for h in chunks:
             for dz in (2, -2):
-                hop(*col_ref(0, c, h), z=zs(dz))
+                hop(col_ref(0, h), far_of(-dz, h), z=zs(dz))
         for h in chunks:
             for dz in (1, -1):
-                hop(col_ref(0, c, h)[0], col_block(0)[1], z=zs(dz))
+                hop(col_ref(0, h), block_of(-dz), z=zs(dz))
         for h, v in pairs:
             for d in (2, 1, -1):
-                leg(*row_ref(0, 0, h), **xs(d))
-                leg(*row_ref(0, 0, v), y=ys(d))
-        twin(col_block(0)[0], 0)
+                leg(row_ref(0, 0, h), leg_of(-d, h), **xs(d))
+                leg(row_ref(0, 0, v), leg_of(-d, v), y=ys(d))
+        twin(C.at[gi], 0)
         for h, v in pairs:
             for d in (2, 1, -1):
-                leg(row_ref(0, 0, v)[0], rest_sem, **xs(d))
-                leg(row_ref(0, 0, h)[0], rest_sem, y=ys(d))
+                leg(row_ref(0, 0, v), rest_sem, **xs(d))
+                leg(row_ref(0, 0, h), rest_sem, y=ys(d))
 
         for step in chunks:
             h, v = pairs[step]
             for d in (1, -1, 2):
                 item = row_ref(0, d, h)
-                arrived(*item)
+                arrived(item, leg_of(d, h))
                 for e in (2, 1, -1):
-                    leg(item[0], rest_sem, y=ys(e))
+                    leg(item, rest_sem, y=ys(e))
                 item = row_ref(d, 0, v)
-                arrived(*item)
+                arrived(item, leg_of(d, v))
                 for e in (2, 1, -1):
-                    leg(item[0], rest_sem, **xs(e))
+                    leg(item, rest_sem, **xs(e))
             for sign in (1, -1):
-                item = col_ref(-2 * sign, c, step)
-                arrived(*item)
+                item = col_ref(-2 * sign, step)
+                arrived(item, far_of(-2 * sign, step))
                 if (step % 2 == 0) == (sign > 0):
-                    hop(item[0], col_block(-2 * sign)[1], z=zs(2 * sign))
-                hop(item[0], col_block(-2 * sign)[1], z=zs(sign))
-                twin(item[0], -2)
+                    hop(item, block_of(4), z=zs(2 * sign))
+                hop(item, block_of(-3 * sign), z=zs(sign))
+                twin(item, -2)
         for dz in (-1, 1) + LATE:
-            item = col_block(dz)
-            arrived(*item)
-            twin(item[0], dz)
+            item = C.at[zs(dz) * 2 + c]
+            arrived(item, block_of(dz))
+            twin(item, dz)
         extra()
         arrived(R.at[pl.ds(0, 12)], rest_sem)
         arrived(C.at[pl.ds(0, len(EARLY))], twin_sem.at[0])
@@ -384,7 +392,7 @@
     tile = pltpu.VMEM((B, B), f32)
     pieces = pltpu.VMEM((N, KP, B), f32)
     strip = pltpu.VMEM((N, B, B), f32)
-    gather_sems = [dma((N, RH)), dma, dma((N, CH)), dma((N,)), dma((2,)), dma, dma]
+    gather_sems = [dma((3, RH)), dma, dma((2, CH)), dma((5,)), dma((2,)), dma, dma]
     return pl.pallas_call(
         kernel,
         out_shape=(pltpu.VMEM((B, B), f32), pltpu.VMEM((B, B), f32)),
@@ -395,7 +403,7 @@
             strip, strip, strip, pltpu.VMEM((N, B + PAD, B), f32),
             pltpu.VMEM((N // 2, 2 * B, 2 * B), jnp.bfloat16),
             tile, tile, tile, tile,
-            dma((2,)), dma, dma((2,)), dma, dma((2,)), dma((4,)), dma, dma((16,)),
+            dma((2,)), dma, dma((2,)), dma, dma((2,)), dma((4,)), dma, dma((9,)),
             *gather_sems, *gather_sems,
         ],
         compiler_params=pltpu.CompilerParams(collective_id=0, has_side_effects=True),

time: 50.4 us -> 48.6 us (0.964)
  Pallas kernels: 48.4 us -> 46.5 us
    pallas_call x1, Pallas kernels: 48.4 us -> 46.5 us  [local(): pl.pallas_call(kernel, out_shape=(pltpu.VMEM((B, B), f32), pltpu.VMEM((B,...]
where the time goes in v6:
time: 48.6 us; the launch traced here: 48.4 us
  Pallas kernels  46.5 us (96%)
  local copies, waits for them, and re-layouts  1.26 us (3%)
  between operations  0.64 us (1%)
    pallas_call x1, Pallas kernels, local(): pl.pallas_call(kernel, out_shape=(pltpu.VMEM((B, B), f32), pltpu.VMEM((B,...  46.5 us
    unnamed x2, local copies, waits for them, and re-layouts  1.26 us

profile of v6, /device:TPU:1, one launch (start us, length us, event | category | flops | bytes accessed | tf_op | source)
XLA Modules:
  0.0 48.4 jit_solution(7197554670135451507)
XLA Ops:
  0.6 46.5 %shard_map.41 = (f32[128,128]{1,0:T(8,128)S(1)}, f32[128,128]{1,0:T(8,128)S(1)}) custom-call(f32[32,128]{1,0:T(8,128)} %bitcast.1, f32[128,128]{1,0:T(8,128)} %a_hbm.1), custom_call_target="tpu_custom_call" | custom-call | tf_op jit(solution)/shard_map/pallas_call | solution.py:396
  47.2 0.6 %copy.6 = f32[128,128]{1,0:T(8,128)} copy(f32[128,128]{1,0:T(8,128)S(1)} %get-tuple-element.2) | data formatting | bytes 131072
  47.8 0.6 %copy.7 = f32[128,128]{1,0:T(8,128)} copy(f32[128,128]{1,0:T(8,128)S(1)} %get-tuple-element.3) | data formatting | bytes 131072

commit v7 on v6

--- a/solution.py
+++ b/solution.py
@@ -32,7 +32,7 @@
 
 
 def kernel(
-    g_hbm, a_hbm, s_out, r_out,
+    g_hbm, a_hbm, both_out,
     a_in, gt, GI, GJ, R1, C1, R2, C2, CB, a_new, s_new, r_own, r_new,
     in_sem, gi_sem, gj_sem, gs_sem, down_sem, swap_sem, piece_sem, send_sem, *gather_sems,
 ):
@@ -47,6 +47,7 @@
     swaps = a != c
 
     sems1, sems2 = gather_sems[:7], gather_sems[7:]
+    s_out, r_out = both_out.at[0], both_out.at[1]
     load_g = pltpu.make_async_copy(g_hbm, gt, in_sem.at[0])
     load_a = pltpu.make_async_copy(a_hbm, a_in, in_sem.at[1])
     load_g.start()
@@ -67,20 +68,22 @@
         to = lax.rem(x + dx + 4, 4)
         return {"b": to // 2, "a": lax.rem(to, 2)}
 
-    def place(slot):
-        return {"y": lax.rem(slot // 2, 4), "b": lax.rem(slot, 2), "c": slot // 8}
+    others = [
+        {"y": ys(dy), "b": pb, "c": pc}
+        for dy in (2, 1, -1, 0) for pb in (b1, b) for pc in (c1, c)
+    ][:-1]
 
     @pl.when(c == 0)
     def _():
-        for t in range(1, N):
-            greet(z=2 * y + b, **place(lax.rem(own + t, N)))
+        for where in others:
+            greet(z=2 * y + b, **where)
 
         @pl.when(jnp.logical_not(home))
         def _():
             greet(z=2 * y + b)
 
-    for t in range(1, N):
-        greet(a=c, **place(lax.rem(own + t, N)))
+    for where in others:
+        greet(a=c, **where)
 
     @pl.when(swaps)
     def _():
@@ -300,8 +303,14 @@
         return jnp.concatenate(split(rows), axis=1)
 
     total = []
+    norms = []
 
     def square(steps):
+        if not norms:
+            norms.append(jnp.zeros((PAD, B), jnp.float32))
+            for k in range(N):
+                block = R1[k]
+                norms[0] = norms[0] + jnp.sum((block * block).reshape(B // PAD, PAD, B), axis=0)
         for dz in steps:
             k = zs(dz)
             CB[k] = columns(C1, k)
@@ -311,14 +320,10 @@
 
     exchange(R1, C1, sems1, B, give_stat, square)
     square(LATE)
-    squares = jnp.zeros((PAD, B), jnp.float32)
-    for k in range(N):
-        block = R1[k]
-        squares = squares + jnp.sum((block * block).reshape(B // PAD, PAD, B), axis=0)
     mid = fold4(sum(total[1:], total[0]))
     R2[gj] = mid
     C2[gi, :B] = mid
-    C2[gi, B:] = squares
+    C2[gi, B:] = norms[0]
 
     def keep_stat():
         @pl.when(swaps)
@@ -393,11 +398,11 @@
     pieces = pltpu.VMEM((N, KP, B), f32)
     strip = pltpu.VMEM((N, B, B), f32)
     gather_sems = [dma((3, RH)), dma, dma((2, CH)), dma((5,)), dma((2,)), dma, dma]
-    return pl.pallas_call(
+    both = pl.pallas_call(
         kernel,
-        out_shape=(pltpu.VMEM((B, B), f32), pltpu.VMEM((B, B), f32)),
+        out_shape=pltpu.VMEM((2, B, B), f32),
         in_specs=[pl.BlockSpec(memory_space=pl.ANY)] * 2,
-        out_specs=[pl.BlockSpec(memory_space=pltpu.VMEM)] * 2,
+        out_specs=pl.BlockSpec(memory_space=pltpu.VMEM),
         scratch_shapes=[
             tile, pltpu.VMEM((KP, B), f32), pieces, pieces,
             strip, strip, strip, pltpu.VMEM((N, B + PAD, B), f32),
@@ -408,6 +413,7 @@
         ],
         compiler_params=pltpu.CompilerParams(collective_id=0, has_side_effects=True),
     )(gradient.T, stat_old)
+    return both[0], both[1]
 
 
 def solution(mesh):

time: 48.6 us -> 48.2 us (level)
  local copies, waits for them, and re-layouts: 1.26 us -> 0.66 us
    unnamed x2 -> x0, local copies, waits for them, and re-layouts: 1.26 us -> none
    squeeze x0 -> x1, local copies, waits for them, and re-layouts: none -> 0.66 us  [local(): return (both[0], both[1])]
where the time goes in v7:
time: 48.2 us; the launch traced here: 48 us
  Pallas kernels  46.7 us (97%)
  local copies, waits for them, and re-layouts  0.66 us (1%)
  between operations  0.64 us (1%)
    pallas_call x1, Pallas kernels, local(): pl.pallas_call(kernel, out_shape=pltpu.VMEM((2, B, B), f32), in_specs=[pl...  46.7 us

profile of v7, /device:TPU:1, one launch (start us, length us, event | category | flops | bytes accessed | tf_op | source)
XLA Modules:
  0.0 48.0 jit_solution(14463415524931835088)
XLA Ops:
  0.6 46.7 %shard_map.41 = f32[2,128,128]{2,1,0:T(8,128)S(1)} custom-call(f32[32,128]{1,0:T(8,128)} %bitcast.5, f32[128,128]{1,0:T(8,128)} %a_hbm.1), custom_call_target="tpu_custom_call" | custom-call | tf_op jit(solution)/shard_map/pallas_call | solution.py:401
  47.4 0.7 %slice_bitcast_fusion = (f32[128,128]{1,0:T(8,128)}, f32[128,128]{1,0:T(8,128)}) fusion(f32[2,128,128]{2,1,0:T(8,128)S(1)} %shard_map.41), kind=kLoop, calls=%fused_computation | loop fusion | bytes 262144 | tf_op jit(solution)/shard_map/squeeze | solution.py:416

commit v8 on v7

--- a/solution.py
+++ b/solution.py
@@ -33,7 +33,7 @@
 
 def kernel(
     g_hbm, a_hbm, both_out,
-    a_in, gt, GI, GJ, R1, C1, R2, C2, CB, a_new, s_new, r_own, r_new,
+    a_in, gt, GI, GJ, R1, C1, R2, C2, CB, held, a_new, s_new, r_own, r_new,
     in_sem, gi_sem, gj_sem, gs_sem, down_sem, swap_sem, piece_sem, send_sem, *gather_sems,
 ):
     z, a = lax.axis_index("z"), lax.axis_index("a")
@@ -178,12 +178,6 @@
 
     send(lower, lower, down_sem.at[0], c == 0, c=c1)
 
-    @pl.when(c == 0)
-    def _():
-        arrived(upper, gj_sem.at[1])
-
-    send(upper, upper, down_sem.at[1], c == 0, c=c1)
-
     @pl.when(a == c)
     def _():
         arrived(GI.at[pl.ds(0, N - 1)], gi_sem)
@@ -193,20 +187,31 @@
         arrived(GI, gi_sem)
         arrived(a_new, swap_sem.at[0])
 
+    def outer(part):
+        left = jnp.transpose(GI[8 * part : 8 * part + 8].reshape(8 * KP, B))
+        right = GJ[8 * part : 8 * part + 8].reshape(8 * KP, B)
+        return fold4(jnp.dot(
+            jnp.concatenate(split(left), axis=0), jnp.concatenate(split(right), axis=1),
+            preferred_element_type=jnp.float32,
+        ))
+
     @pl.when(c == 1)
     def _():
         arrived(lower, down_sem.at[0])
+
+    held[0] = outer(0)
+
+    @pl.when(c == 0)
+    def _():
+        arrived(upper, gj_sem.at[1])
+
+    send(upper, upper, down_sem.at[1], c == 0, c=c1)
+
+    @pl.when(c == 1)
+    def _():
         arrived(upper, down_sem.at[1])
 
-    left = jnp.transpose(GI[...].reshape(N * KP, B))
-    right = GJ[...].reshape(N * KP, B)
-    lh, ll = split(left)
-    rh, rl = split(right)
-    full = jnp.dot(
-        jnp.concatenate([lh, ll], axis=0), jnp.concatenate([rh, rl], axis=1),
-        preferred_element_type=jnp.float32,
-    )
-    stat = 0.9 * a_new[...] + fold4(full) / float(N * KP)
+    stat = 0.9 * a_new[...] + (held[0] + outer(1)) / float(N * KP)
     R1[gj] = stat
     C1[gi] = stat
 
@@ -317,10 +322,13 @@
             total.append(jnp.dot(
                 jnp.concatenate(strips(R1, k), axis=0), CB[k], preferred_element_type=jnp.float32
             ))
+        if steps == EARLY:
+            held[0] = fold4(sum(total[1:], total[0]))
 
     exchange(R1, C1, sems1, B, give_stat, square)
+    early = len(EARLY)
     square(LATE)
-    mid = fold4(sum(total[1:], total[0]))
+    mid = held[0] + fold4(sum(total[early + 1 :], total[early]))
     R2[gj] = mid
     C2[gi, :B] = mid
     C2[gi, B:] = norms[0]
@@ -349,7 +357,17 @@
                     jnp.concatenate([hi[cut], lo[cut]], axis=0), both, preferred_element_type=jnp.float32
                 ))
 
-    exchange(R2, C2, sems2, B + PAD, keep_stat, lambda steps: powers(steps, (0, 1)))
+    def fold2(full):
+        return (full[:half, :B] + full[half:, :B]) + (full[:half, B:] + full[half:, B:])
+
+    def first_powers(steps):
+        powers(steps, (0, 1))
+        for part in (0, 1):
+            full = sum(wide[part][1:], wide[part][0])
+            held[0, part * half : part * half + half] = fold2(full[:, : 2 * B])
+            held[1, part * half : part * half + half] = fold2(full[:, 2 * B:])
+
+    exchange(R2, C2, sems2, B + PAD, keep_stat, first_powers)
 
     squares = jnp.zeros((PAD, B), jnp.float32)
     for k in range(N):
@@ -359,15 +377,12 @@
     rows = lax.broadcasted_iota(jnp.int32, (half, B), 0) + gi * B
     cols = lax.broadcasted_iota(jnp.int32, (half, B), 1) + gj * B
 
-    def fold2(full):
-        return (full[:half, :B] + full[half:, :B]) + (full[:half, B:] + full[half:, B:])
-
     for part in (0, 1):
         powers(LATE, (part,))
-        full = sum(wide[part][1:], wide[part][0])
-        cube = fold2(full[:, : 2 * B])
-        quad = fold2(full[:, 2 * B:])
+        full = sum(wide[part][early + 1 :], wide[part][early])
         cut = pl.ds(part * half, half)
+        cube = held[0, cut] + fold2(full[:, : 2 * B])
+        quad = held[1, cut] + fold2(full[:, 2 * B:])
         eye = jnp.where(rows + part * half == cols, A0, 0.0)
         tail = A2 * R2[gj, cut] + inv * (A3 * cube + inv * (A4 * quad))
         r_own[cut] = eye + inv * (A1 * R1[gj, cut] + inv * tail)
@@ -407,6 +422,7 @@
             tile, pltpu.VMEM((KP, B), f32), pieces, pieces,
             strip, strip, strip, pltpu.VMEM((N, B + PAD, B), f32),
             pltpu.VMEM((N // 2, 2 * B, 2 * B), jnp.bfloat16),
+            pltpu.VMEM((2, B, B), f32),
             tile, tile, tile, tile,
             dma((2,)), dma, dma((2,)), dma, dma((2,)), dma((4,)), dma, dma((9,)),
             *gather_sems, *gather_sems,

time: 48.2 us -> 47.6 us (0.988)
  Pallas kernels: 46.7 us -> 46.1 us
    pallas_call x1, Pallas kernels: 46.7 us -> 46.1 us  [local(): pl.pallas_call(kernel, out_shape=pltpu.VMEM((2, B, B), f32), in_specs=[pl...]
where the time goes in v8:
time: 47.6 us; the launch traced here: 47.4 us
  Pallas kernels  46.1 us (97%)
  local copies, waits for them, and re-layouts  0.66 us (1%)
  between operations  0.64 us (1%)
    pallas_call x1, Pallas kernels, local(): pl.pallas_call(kernel, out_shape=pltpu.VMEM((2, B, B), f32), in_specs=[pl...  46.1 us

profile of v8, /device:TPU:1, one launch (start us, length us, event | category | flops | bytes accessed | tf_op | source)
XLA Modules:
  0.0 47.4 jit_solution(12602665878327875503)
XLA Ops:
  0.6 46.1 %shard_map.41 = f32[2,128,128]{2,1,0:T(8,128)S(1)} custom-call(f32[32,128]{1,0:T(8,128)} %bitcast.5, f32[128,128]{1,0:T(8,128)} %a_hbm.1), custom_call_target="tpu_custom_call" | custom-call | tf_op jit(solution)/shard_map/pallas_call | solution.py:416
  46.8 0.7 %slice_bitcast_fusion = (f32[128,128]{1,0:T(8,128)}, f32[128,128]{1,0:T(8,128)}) fusion(f32[2,128,128]{2,1,0:T(8,128)S(1)} %shard_map.41), kind=kLoop, calls=%fused_computation | loop fusion | bytes 262144 | tf_op jit(solution)/shard_map/squeeze | solution.py:432

commit v9 on v8

--- a/solution.py
+++ b/solution.py
@@ -333,6 +333,8 @@
     C2[gi, :B] = mid
     C2[gi, B:] = norms[0]
 
+    drained = []
+
     def keep_stat():
         @pl.when(swaps)
         def _():
@@ -342,6 +344,12 @@
         @pl.when(a == c)
         def _():
             s_out[...] = R1[gj]
+
+        left_here(R1.at[pl.ds(0, 11), pl.ds(0, 2 * KP)], piece_sem)
+        sent(R1, C1, sems1)
+        for copy, cond in sends:
+            pl.when(cond)(copy.wait_send)
+        drained.append(len(sends))
 
     half = B // 2
     wide = [[], []]
@@ -388,6 +396,8 @@
         r_own[cut] = eye + inv * (A1 * R1[gj, cut] + inv * tail)
         send(r_own.at[cut], r_new.at[cut], swap_sem.at[2 + part], swaps, a=a1, c=c1)
 
+    sent(R2, C2, sems2)
+
     @pl.when(swaps)
     def _():
         for part in (0, 1):
@@ -399,10 +409,7 @@
     def _():
         r_out[...] = r_own[...]
 
-    left_here(R1.at[pl.ds(0, 11), pl.ds(0, 2 * KP)], piece_sem)
-    sent(R1, C1, sems1)
-    sent(R2, C2, sems2)
-    for copy, cond in sends:
+    for copy, cond in sends[drained[0]:]:
         pl.when(cond)(copy.wait_send)
 
 

time: 47.6 us -> 47.6 us (level)
  no operation moved by 1% of the time
where the time goes in v9:
time: 47.6 us; the launch traced here: 47.4 us
  Pallas kernels  46.1 us (97%)
  local copies, waits for them, and re-layouts  0.66 us (1%)
  between operations  0.64 us (1%)
    pallas_call x1, Pallas kernels, local(): pl.pallas_call(kernel, out_shape=pltpu.VMEM((2, B, B), f32), in_specs=[pl...  46.1 us

profile of v9, /device:TPU:1, one launch (start us, length us, event | category | flops | bytes accessed | tf_op | source)
XLA Modules:
  0.0 47.4 jit_solution(9592314678130387825)
XLA Ops:
  0.6 46.1 %shard_map.41 = f32[2,128,128]{2,1,0:T(8,128)S(1)} custom-call(f32[32,128]{1,0:T(8,128)} %bitcast.5, f32[128,128]{1,0:T(8,128)} %a_hbm.1), custom_call_target="tpu_custom_call" | custom-call | tf_op jit(solution)/shard_map/pallas_call | solution.py:423
  46.8 0.7 %slice_bitcast_fusion = (f32[128,128]{1,0:T(8,128)}, f32[128,128]{1,0:T(8,128)}) fusion(f32[2,128,128]{2,1,0:T(8,128)S(1)} %shard_map.41), kind=kLoop, calls=%fused_computation | loop fusion | bytes 262144 | tf_op jit(solution)/shard_map/squeeze | solution.py:439

commit v10 on v8

--- a/solution.py
+++ b/solution.py
@@ -267,7 +267,7 @@
 
         for step in chunks:
             h, v = pairs[step]
-            for d in (1, -1, 2):
+            for d in (1, -1):
                 item = row_ref(0, d, h)
                 arrived(item, leg_of(d, h))
                 for e in (2, 1, -1):
@@ -283,12 +283,21 @@
                     hop(item, block_of(4), z=zs(2 * sign))
                 hop(item, block_of(-3 * sign), z=zs(sign))
                 twin(item, -2)
+            for d in (2,):
+                item = row_ref(0, d, h)
+                arrived(item, leg_of(d, h))
+                for e in (2, 1, -1):
+                    leg(item, rest_sem, y=ys(e))
+                item = row_ref(d, 0, v)
+                arrived(item, leg_of(d, v))
+                for e in (2, 1, -1):
+                    leg(item, rest_sem, **xs(e))
         for dz in (-1, 1) + LATE:
             item = C.at[zs(dz) * 2 + c]
             arrived(item, block_of(dz))
             twin(item, dz)
+        arrived(R.at[pl.ds(0, 12)], rest_sem)
         extra()
-        arrived(R.at[pl.ds(0, 12)], rest_sem)
         arrived(C.at[pl.ds(0, len(EARLY))], twin_sem.at[0])
         ready(EARLY)
         arrived(C.at[pl.ds(0, len(LATE))], twin_sem.at[1])

time: 47.6 us -> 47.6 us (level)
  no operation moved by 1% of the time
where the time goes in v10:
time: 47.6 us; the launch traced here: 47.4 us
  Pallas kernels  46.1 us (97%)
  local copies, waits for them, and re-layouts  0.66 us (1%)
  between operations  0.64 us (1%)
    pallas_call x1, Pallas kernels, local(): pl.pallas_call(kernel, out_shape=pltpu.VMEM((2, B, B), f32), in_specs=[pl...  46.1 us

profile of v10, /device:TPU:1, one launch (start us, length us, event | category | flops | bytes accessed | tf_op | source)
XLA Modules:
  0.0 47.4 jit_solution(16624118477830989236)
XLA Ops:
  0.6 46.1 %shard_map.41 = f32[2,128,128]{2,1,0:T(8,128)S(1)} custom-call(f32[32,128]{1,0:T(8,128)} %bitcast.5, f32[128,128]{1,0:T(8,128)} %a_hbm.1), custom_call_target="tpu_custom_call" | custom-call | tf_op jit(solution)/shard_map/pallas_call | solution.py:425
  46.8 0.7 %slice_bitcast_fusion = (f32[128,128]{1,0:T(8,128)}, f32[128,128]{1,0:T(8,128)}) fusion(f32[2,128,128]{2,1,0:T(8,128)S(1)} %shard_map.41), kind=kLoop, calls=%fused_computation | loop fusion | bytes 262144 | tf_op jit(solution)/shard_map/squeeze | solution.py:441

commit v11 on v8

--- a/solution.py
+++ b/solution.py
@@ -343,7 +343,7 @@
         def _():
             s_out[...] = R1[gj]
 
-    half = B // 2
+    spans = ((0, 96), (96, 32))
     wide = [[], []]
 
     def powers(steps, halves):
@@ -352,20 +352,21 @@
                 k = zs(dz)
                 both = jnp.concatenate([CB[k], columns(C2, k)], axis=1)
                 hi, lo = strips(R2, k)
-                cut = slice(part * half, part * half + half)
+                cut = slice(spans[part][0], sum(spans[part]))
                 wide[part].append(jnp.dot(
                     jnp.concatenate([hi[cut], lo[cut]], axis=0), both, preferred_element_type=jnp.float32
                 ))
 
     def fold2(full):
+        half = full.shape[0] // 2
         return (full[:half, :B] + full[half:, :B]) + (full[:half, B:] + full[half:, B:])
 
     def first_powers(steps):
         powers(steps, (0, 1))
         for part in (0, 1):
             full = sum(wide[part][1:], wide[part][0])
-            held[0, part * half : part * half + half] = fold2(full[:, : 2 * B])
-            held[1, part * half : part * half + half] = fold2(full[:, 2 * B:])
+            held[0, spans[part][0] : sum(spans[part])] = fold2(full[:, : 2 * B])
+            held[1, spans[part][0] : sum(spans[part])] = fold2(full[:, 2 * B:])
 
     exchange(R2, C2, sems2, B + PAD, keep_stat, first_powers)
 
@@ -374,16 +375,16 @@
         squares = squares + C2[k, B:]
     whole = jnp.sum(squares, keepdims=True)
     inv = 1.0 / (2.0 * jnp.sqrt(whole / float(N * B)))
-    rows = lax.broadcasted_iota(jnp.int32, (half, B), 0) + gi * B
-    cols = lax.broadcasted_iota(jnp.int32, (half, B), 1) + gj * B
+    rows = lax.broadcasted_iota(jnp.int32, (B, B), 0) + gi * B
+    cols = lax.broadcasted_iota(jnp.int32, (B, B), 1) + gj * B
 
     for part in (0, 1):
         powers(LATE, (part,))
         full = sum(wide[part][early + 1 :], wide[part][early])
-        cut = pl.ds(part * half, half)
+        cut = pl.ds(*spans[part])
         cube = held[0, cut] + fold2(full[:, : 2 * B])
         quad = held[1, cut] + fold2(full[:, 2 * B:])
-        eye = jnp.where(rows + part * half == cols, A0, 0.0)
+        eye = jnp.where(rows == cols, A0, 0.0)[spans[part][0] : sum(spans[part])]
         tail = A2 * R2[gj, cut] + inv * (A3 * cube + inv * (A4 * quad))
         r_own[cut] = eye + inv * (A1 * R1[gj, cut] + inv * tail)
         send(r_own.at[cut], r_new.at[cut], swap_sem.at[2 + part], swaps, a=a1, c=c1)
@@ -391,7 +392,7 @@
     @pl.when(swaps)
     def _():
         for part in (0, 1):
-            cut = pl.ds(part * half, half)
+            cut = pl.ds(*spans[part])
             arrived(r_new.at[cut], swap_sem.at[2 + part])
             r_out[cut] = r_new[cut]
 

time: 47.6 us -> 47.7 us (level)
  no operation moved by 1% of the time
where the time goes in v11:
time: 47.7 us; the launch traced here: 47.6 us
  Pallas kernels  46.3 us (97%)
  local copies, waits for them, and re-layouts  0.66 us (1%)
  between operations  0.64 us (1%)
    pallas_call x1, Pallas kernels, local(): pl.pallas_call(kernel, out_shape=pltpu.VMEM((2, B, B), f32), in_specs=[pl...  46.3 us

profile of v11, /device:TPU:1, one launch (start us, length us, event | category | flops | bytes accessed | tf_op | source)
XLA Modules:
  0.0 47.6 jit_solution(11220589971346953555)
XLA Ops:
  0.6 46.3 %shard_map.41 = f32[2,128,128]{2,1,0:T(8,128)S(1)} custom-call(f32[32,128]{1,0:T(8,128)} %bitcast.5, f32[128,128]{1,0:T(8,128)} %a_hbm.1), custom_call_target="tpu_custom_call" | custom-call | tf_op jit(solution)/shard_map/pallas_call | solution.py:417
  46.9 0.7 %slice_bitcast_fusion = (f32[128,128]{1,0:T(8,128)}, f32[128,128]{1,0:T(8,128)}) fusion(f32[2,128,128]{2,1,0:T(8,128)S(1)} %shard_map.41), kind=kLoop, calls=%fused_computation | loop fusion | bytes 262144 | tf_op jit(solution)/shard_map/squeeze | solution.py:433
